TPU v7x, 128 devices: a whole 4x4x4 slice. The times are simulated.
128 devices in a mesh: dev: 128 (over x, z, y, core).
Axes of the slice: x: 4, y: 4, z: 4, core: 2. Of those that a mesh axis runs over, the one named last changes fastest.
Arguments:
- pixels: float32 [4, 2048, 8192], P(None, 'dev'), may hold values from -10 to 10
- valid_flags: int32 [4, 2048, 8192], P(None, 'dev'), may hold values 0 or 1
Outputs:
- tile_halves: float32 [128, 256, 2048], P('dev')
- header: float32 [5, 4], replicated
All inputs are finite; a program needn't handle non-finite values. No bound on the sum of `valid_flags` on one device may be relied on, other than what follows from the above.
Results may differ from a plain program's by a relative error of at most 0.00002.
Values sent between devices are 32-bit elements; how exact they have to be, the bound alone decides.
No kernel may reach another device: no remote copies, remote signals or barrier semaphores. Data moves between devices by JAX's collectives and lax.ppermute only.
A program may use at most 128 MiB of HBM per device.

v0:
```python
import jax
import jax.numpy as jnp
from jax import lax
from jax.sharding import Mesh
from jax.sharding import PartitionSpec as P

TILE = 512
DEV = ("dev_0", "dev_1", "dev_2", "dev_3")


largest_value = 3e38


def from_partner(value, axis, stride):
    mask = 2**stride
    pairs = [(source, source ^ mask) for source in range(lax.axis_size(axis))]
    return lax.ppermute(value, axis, pairs)


def gathered_once(x, axis):
    leaves = jax.tree.leaves(x)
    sequence = sorted(range(len(leaves)), key=lambda k: -leaves[k].size)
    width = (1, *leaves[sequence[0]].shape)[-1]
    lines = [
        jnp.pad(leaves[k].reshape(-1), (0, -leaves[k].size % width)).reshape(-1, width)
        for k in sequence
    ]
    both, at, found = (lax.all_gather(jnp.concatenate(lines), axis), 0, {})
    for k, line in zip(sequence, lines):
        section = both[:, at : at + len(line)].reshape(len(both), -1)
        found[k] = section[:, : leaves[k].size].reshape(-1, *leaves[k].shape)
        at += len(line)
    numbers = iter(range(len(leaves)))
    return jax.tree.map(lambda _: found[next(numbers)], x)


def merged_by_axis(x, axes, combine):
    for axis in axes:
        pieces = gathered_once(x, axis)
        x = jax.tree.map(lambda part: part[0], pieces)
        for k in range(1, lax.axis_size(axis)):
            x = combine(x, jax.tree.map(lambda part: part[k], pieces))
    return x


def combine_centred(earlier, later):
    merged_count = earlier[2] + later[2]
    mean_gap = later[3] - earlier[3]
    weight = later[2] / jnp.maximum(merged_count, 1.0)
    return (
        jnp.minimum(earlier[0], later[0]),
        jnp.maximum(earlier[1], later[1]),
        merged_count,
        earlier[3] + mean_gap * weight,
        earlier[4] + later[4] + mean_gap * mean_gap * earlier[2] * weight,
    )


def section_split(result, position, bit_index, members):
    own_bit = position >> bit_index & 1
    paired = result.reshape((members >> bit_index + 1, 2, 1 << bit_index) + result.shape[1:])
    lower_half = paired[:, 0]
    upper_half = paired[:, 1]
    outgoing = jnp.where(own_bit == 1, lower_half, upper_half)
    return (own_bit, lower_half, upper_half, outgoing)


def section_join(result, own_bit, lower_half, upper_half, incoming):
    new_lower = jnp.where(own_bit == 1, incoming, lower_half)
    new_upper = jnp.where(own_bit == 1, upper_half, incoming)
    return jnp.stack([new_lower, new_upper], axis=1).reshape(result.shape)


def on_device(pixels, valid_flags):
    band_total, strip_rows, columns = pixels.shape
    members = columns // TILE
    usable = valid_flags == 1
    filled = jnp.where(usable, pixels, jnp.float32(0.0))
    pieces = jnp.transpose(filled.reshape(band_total, strip_rows, members, TILE), (2, 1, 3, 0))
    pieces = pieces.reshape(members, strip_rows, TILE * band_total)
    position = lax.axis_index(DEV) % members
    section_count = members.bit_length() - 1
    result = pieces
    for bit_index in range(section_count):
        own_bit, lower_half, upper_half, outgoing = section_split(
            result, position, bit_index, members
        )
        incoming = from_partner(outgoing, DEV, bit_index)
        result = section_join(result, own_bit, lower_half, upper_half, incoming)
    tile_halves = result.reshape(1, members * strip_rows, TILE * band_total)
    lowest = jnp.min(jnp.where(usable, pixels, jnp.float32(largest_value)), axis=(1, 2))
    highest = jnp.max(jnp.where(usable, pixels, jnp.float32(-largest_value)), axis=(1, 2))
    valid_count = jnp.sum(usable.astype(jnp.float32), axis=(1, 2))
    band_sum = jnp.sum(filled, axis=(1, 2))
    local_mean = band_sum / jnp.maximum(valid_count, 1.0)
    deviation = jnp.where(usable, pixels - local_mean[:, None, None], jnp.float32(0.0))
    spread = jnp.sum(deviation * deviation, axis=(1, 2))
    merged = merged_by_axis(
        (lowest, highest, valid_count, local_mean, spread), DEV, combine_centred
    )
    average = merged[3]
    variance = merged[4] / jnp.maximum(merged[2], 1.0)
    cell_total = strip_rows * columns * lax.axis_size(DEV)
    header = jnp.stack(
        [
            merged[0],
            merged[1],
            merged[2] / cell_total,
            average,
            jnp.sqrt(jnp.maximum(variance, 0.25)),
        ]
    )
    return (tile_halves, header)


def solution(mesh):
    split = Mesh(mesh.devices.reshape(4, 4, 4, 2), ("dev_0", "dev_1", "dev_2", "dev_3"))
    placed = (P(None, DEV, None), P(None, DEV, None))
    return jax.shard_map(
        on_device, mesh=split, in_specs=placed, out_specs=(P(DEV, None, None), P()), check_vma=False
    )
```

profile of v0, /device:TPU:0, one launch (start us, length us, event | category | flops | bytes accessed | tf_op | source)
XLA Modules:
  0.0 147.9 jit_solution(4155668410068421382)
XLA Ops:
  0.6 2.2 %convert_reduce_fusion = (f32[4]{0:T(128)S(1)}, pred[4,16,8192]{2,1,0:T(8,128)(4,1)S(1)}) fusion(s32[4,16,8192]{2,1,0:T(8,128)} %param.3), kind=kLoop, calls=%fused_computation.11 | loop fusion | flops 1572860 | bytes 2621456 | tf_op jit(solution)/shard_map/reduce_sum | solution.py:93
  2.8 2.0 %fusion.31 = (f32[4]{0:T(128)S(1)}, f32[4,16,8192]{2,1,0:T(8,128)S(1)}) fusion(pred[4,16,8192]{2,1,0:T(8,128)(4,1)S(1)} %get-tuple-element.57, f32[4,16,8192]{2,1,0:T(8,128)} %param.2), kind=kLoop, calls=%fused_computation.172 | loop fusion | flops 1048572 | bytes 4718608 | tf_op jit(solution)/shard_map/reduce_sum | solution.py:94
  4.8 10.7 %copy.51 = f32[4,16,8192]{1,0,2:T(4,128)} copy(f32[4,16,8192]{2,1,0:T(8,128)S(1)} %get-tuple-element.59) | data formatting | bytes 4194304 | tf_op jit(solution)/shard_map/reshape | solution.py:79
  15.5 9.8 %fusion.1 = f32[8,1,16,2048]{2,3,0,1:T(8,128)} fusion(f32[8,2,1,16,2048]{3,4,1,0,2:T(8,128)} %bitcast.544, pred[]{:T(512)S(6)} %eq.31), kind=kLoop, calls=%fused_computation.3 | loop fusion | flops 262144 | bytes 3145729 | tf_op jit(solution)/shard_map/jit(_where)/select_n | solution.py:64
  25.4 5.1 %copy.37 = f32[8,1,16,2048]{3,2,1,0:T(8,128)S(1)} copy(f32[8,1,16,2048]{2,3,0,1:T(8,128)} %fusion.1) | data formatting | bytes 2097152 | tf_op jit(solution)/shard_map/jit(_where)/select_n | solution.py:64
  30.6 2.6 %collective-permute-done = f32[8,1,16,2048]{3,2,1,0:T(8,128)S(1)} collective-permute-done((f32[8,1,16,2048]{3,2,1,0:T(8,128)S(1)}, f32[8,1,16,2048]{3,2,1,0:T(8,128)S(1)}, u32[]{:S(2)}, u32[]{:S(2)}) %collective-permute-start) | collective-permute-done | bytes 1048608 | tf_op jit(solution)/shard_map/ppermute | solution.py:17
  33.2 4.6 %copy.38 = f32[8,1,16,2048]{2,3,0,1:T(8,128)} copy(f32[8,1,16,2048]{3,2,1,0:T(8,128)S(1)} %collective-permute-done) | data formatting | bytes 2097152 | tf_op jit(solution)/shard_map/ppermute | solution.py:17
  37.8 15.1 %fusion = (f32[8,1,16,2048]{2,3,0,1:T(8,128)}, f32[8,1,16,2048]{2,3,0,1:T(8,128)}) fusion(f32[8,1,16,2048]{2,3,0,1:T(8,128)} %copy.38, f32[8,2,1,16,2048]{3,4,1,0,2:T(8,128)} %bitcast.545, pred[]{:T(512)S(6)} %eq.31), kind=kLoop, calls=%fused_computation.2 | loop fusion | flops 524288 | bytes 5242881 | tf_op jit(solution)/shard_map/jit(_where)/select_n | solution.py:69
  52.9 5.1 %copy.39 = f32[8,1,16,2048]{3,2,0,1:T(8,128)S(1)} copy(f32[8,1,16,2048]{2,3,0,1:T(8,128)} %get-tuple-element.60) | data formatting | bytes 2097152 | tf_op jit(solution)/shard_map/jit(_where)/select_n | solution.py:69
  58.0 5.1 %copy.41 = f32[8,1,16,2048]{3,2,0,1:T(8,128)S(1)} copy(f32[8,1,16,2048]{2,3,0,1:T(8,128)} %get-tuple-element.61) | data formatting | bytes 2097152 | tf_op jit(solution)/shard_map/jit(_where)/select_n | solution.py:70
  64.2 1.7 %collective-permute-start.1 = (f32[4,2,16,2048]{3,2,0,1:T(8,128)}, f32[4,2,16,2048]{3,2,0,1:T(8,128)}, u32[]{:S(2)}, u32[]{:S(2)}) collective-permute-start(f32[4,2,16,2048]{3,2,0,1:T(8,128)} %broadcast_select_fusion.1), channel_id=1, source_target_pairs={{0,2},{1,3},{2,0},{3,1},{4,6},{5,7},{6,4},{7,5},{8,10},{9,11},{10,... | collective-permute-start | bytes 3145736 | tf_op jit(solution)/shard_map/ppermute | solution.py:17
  65.9 23.8 %collective-permute-done.1 = f32[4,2,16,2048]{3,2,0,1:T(8,128)} collective-permute-done((f32[4,2,16,2048]{3,2,0,1:T(8,128)}, f32[4,2,16,2048]{3,2,0,1:T(8,128)}, u32[]{:S(2)}, u32[]{:S(2)}) %collective-permute-start.1) | collective-permute-done | bytes 1048608 | tf_op jit(solution)/shard_map/ppermute | solution.py:17
  89.7 1.4 select_bitcast_fusion.5
  92.6 3.3 %collective-permute-start.2 = (f32[2,4,16,2048]{3,2,1,0:T(8,128)}, f32[2,4,16,2048]{3,2,1,0:T(8,128)}, u32[]{:S(2)}, u32[]{:S(2)}) collective-permute-start(f32[2,4,16,2048]{3,2,1,0:T(8,128)} %fusion.6), channel_id=1, source_target_pairs={{0,4},{1,5},{2,6},{3,7},{4,0},{5,1},{6,2},{7,3},{8,12},{9,13},{10,... | collective-permute-start | bytes 3145736 | tf_op jit(solution)/shard_map/ppermute | solution.py:17
  95.9 1.3 multiply_reduce_fusion
  97.4 11.2 %all-gather.4 = f32[4,5,4]{1,2,0:T(4,128)S(1)} all-gather(f32[1,5,4]{1,2,0:T(4,128)S(1)} %bitcast.558), channel_id=2, replica_groups=mesh['dev_0'=4,'dev_1'=4,'dev_2'=4,'dev_3'=2] {'dev_0'}, dimensions={0}, use_global_device_ids=true | all-gather | bytes 400 | tf_op jit(solution)/shard_map/all_gather | solution.py:28
  109.2 12.0 %all-gather.5 = f32[4,5,4]{1,2,0:T(4,128)S(1)} all-gather(f32[1,5,4]{1,2,0:T(4,128)S(1)} %bitcast.557), channel_id=3, replica_groups=mesh['dev_0'=4,'dev_1'=4,'dev_2'=4,'dev_3'=2] {'dev_1'}, dimensions={0}, use_global_device_ids=true | all-gather | bytes 400 | tf_op jit(solution)/shard_map/all_gather | solution.py:28
  121.6 1.7 %select_bitcast_fusion.3 = (f32[2,1,4,16,2048]{4,3,2,0,1:T(8,128)S(1)}, f32[2,1,4,16,2048]{4,3,2,0,1:T(8,128)S(1)}) fusion(f32[2,4,16,2048]{3,2,1,0:T(8,128)} %collective-permute-done.2, pred[]{:T(512)S(6)} %eq.15, f32[2,2,4,16,2048]{4,3,2,1,0:T(8,128)} %bitcast.555, f32[2,2,4,16,2048]{4,3,1,0,2:T(8,128)S(1)} %bitcast.549), kind=kLoop, calls=%fused_computation.25 | loop fusion | flops 524288 | bytes 5242881 | tf_op jit(solution)/shard_map/stack | solution.py:71
  123.9 1.7 %collective-permute-start.3 = (f32[1,8,16,2048]{3,2,1,0:T(8,128)S(1)}, f32[1,8,16,2048]{3,2,1,0:T(8,128)}, u32[]{:S(2)}, u32[]{:S(2)}) collective-permute-start(f32[1,8,16,2048]{3,2,1,0:T(8,128)S(1)} %fusion.7), channel_id=1, source_target_pairs={{0,8},{1,9},{2,10},{3,11},{4,12},{5,13},{6,14},{7,15},{8,0},{9,1},... | collective-permute-start | bytes 3145736 | tf_op jit(solution)/shard_map/ppermute | solution.py:17
  126.0 10.4 %all-gather.6 = f32[4,5,4]{1,2,0:T(4,128)S(1)} all-gather(f32[1,5,4]{1,2,0:T(4,128)S(1)} %bitcast.559), channel_id=4, replica_groups=mesh['dev_0'=4,'dev_1'=4,'dev_2'=4,'dev_3'=2] {'dev_2'}, dimensions={0}, use_global_device_ids=true | all-gather | bytes 400 | tf_op jit(solution)/shard_map/all_gather | solution.py:28
  137.1 1.8 %all-gather.7 = f32[2,5,4]{1,2,0:T(4,128)S(1)} all-gather(f32[1,5,4]{1,2,0:T(4,128)S(1)} %bitcast.560), channel_id=5, replica_groups=mesh['dev_0'=4,'dev_1'=4,'dev_2'=4,'dev_3'=2] {'dev_3'}, dimensions={0}, use_global_device_ids=true | all-gather | bytes 240 | tf_op jit(solution)/shard_map/all_gather | solution.py:28
  140.0 5.1 %collective-permute-done.3 = f32[1,8,16,2048]{3,2,1,0:T(8,128)} collective-permute-done((f32[1,8,16,2048]{3,2,1,0:T(8,128)S(1)}, f32[1,8,16,2048]{3,2,1,0:T(8,128)}, u32[]{:S(2)}, u32[]{:S(2)}) %collective-permute-start.3) | collective-permute-done | bytes 1048608 | tf_op jit(solution)/shard_map/ppermute | solution.py:17
  145.0 1.4 select_bitcast_fusion.1
  146.5 1.5 pad_maximum_fusion.2
  (36 shorter events, 6.4 us)
Async XLA Ops:
  30.5 2.7 %collective-permute-start = (f32[8,1,16,2048]{3,2,1,0:T(8,128)S(1)}, f32[8,1,16,2048]{3,2,1,0:T(8,128)S(1)}, u32[]{:S(2)}, u32[]{:S(2)}) collective-permute-start(f32[8,1,16,2048]{3,2,1,0:T(8,128)S(1)} %copy.37), channel_id=1, source_target_pairs={{0,1},{1,0},{2,3},{3,2},{4,5},{5,4},{6,7},{7,6},{8,9},{9,8},{10,11... | collective-permute-start | bytes 3145736 | tf_op jit(solution)/shard_map/ppermute | solution.py:17
  64.2 25.5 %collective-permute-start.1 = (f32[4,2,16,2048]{3,2,0,1:T(8,128)}, f32[4,2,16,2048]{3,2,0,1:T(8,128)}, u32[]{:S(2)}, u32[]{:S(2)}) collective-permute-start(f32[4,2,16,2048]{3,2,0,1:T(8,128)} %broadcast_select_fusion.1), channel_id=1, source_target_pairs={{0,2},{1,3},{2,0},{3,1},{4,6},{5,7},{6,4},{7,5},{8,10},{9,11},{10,... | collective-permute-start | bytes 3145736 | tf_op jit(solution)/shard_map/ppermute | solution.py:17
  91.4 5.8 %copy-start.1 = (f32[4,2,2,16,2048]{4,3,2,1,0:T(8,128)}, f32[4,2,2,16,2048]{4,3,2,1,0:T(8,128)S(1)}, u32[]{:S(2)}) copy-start(f32[4,2,2,16,2048]{4,3,2,1,0:T(8,128)S(1)} %copy.43) | copy-start | bytes 6291460
  91.4 4.5 %copy-start = (f32[4,16,8192]{2,1,0:T(8,128)S(1)}, f32[4,16,8192]{2,1,0:T(8,128)}, u32[]{:S(2)}) copy-start(f32[4,16,8192]{2,1,0:T(8,128)} %param.2) | copy-start | bytes 6291460
  92.6 29.0 %collective-permute-start.2 = (f32[2,4,16,2048]{3,2,1,0:T(8,128)}, f32[2,4,16,2048]{3,2,1,0:T(8,128)}, u32[]{:S(2)}, u32[]{:S(2)}) collective-permute-start(f32[2,4,16,2048]{3,2,1,0:T(8,128)} %fusion.6), channel_id=1, source_target_pairs={{0,4},{1,5},{2,6},{3,7},{4,0},{5,1},{6,2},{7,3},{8,12},{9,13},{10,... | collective-permute-start | bytes 3145736 | tf_op jit(solution)/shard_map/ppermute | solution.py:17
  123.9 21.1 %collective-permute-start.3 = (f32[1,8,16,2048]{3,2,1,0:T(8,128)S(1)}, f32[1,8,16,2048]{3,2,1,0:T(8,128)}, u32[]{:S(2)}, u32[]{:S(2)}) collective-permute-start(f32[1,8,16,2048]{3,2,1,0:T(8,128)S(1)} %fusion.7), channel_id=1, source_target_pairs={{0,8},{1,9},{2,10},{3,11},{4,12},{5,13},{6,14},{7,15},{8,0},{9,1},... | collective-permute-start | bytes 3145736 | tf_op jit(solution)/shard_map/ppermute | solution.py:17
where the time goes:
time: 148 us
  other arithmetic  40.7 us (28%)
  blocking collectives  35.4 us (24%)
  local copies, waits for them, and re-layouts  32.7 us (22%)
  waiting for transfers between devices  31.5 us (21%)
  starting transfers between devices  6.78 us (5%)
    all_gather x4, blocking collectives, gathered_once(): both, at, found = (lax.all_gather(jnp.concatenate(lines), axis), 0, {})  35.4 us
    ppermute x4, waiting for transfers between devices, from_partner(): return lax.ppermute(value, axis, pairs)  31.5 us
    select_n x1, other arithmetic, section_join(): new_lower = jnp.where(own_bit == 1, incoming, lower_half)  15.1 us
    select_n x4, other arithmetic, section_split(): outgoing = jnp.where(own_bit == 1, lower_half, upper_half)  12.2 us
    reshape x1, local copies, waits for them, and re-layouts, on_device(): filled.reshape(band_total, strip_rows, members, TILE)  10.7 us
    ppermute x4, starting transfers between devices, from_partner(): return lax.ppermute(value, axis, pairs)  6.78 us
    another operation x6, other arithmetic, section_join(): return jnp.stack([new_lower, new_upper], axis=1).reshape(result.shape)  6.38 us
    select_n x1, local copies, waits for them, and re-layouts, section_join(): new_upper = jnp.where(own_bit == 1, upper_half, incoming)  5.12 us
  transfers between devices with their start and end apart: 4, of which 3 were waited for; matrix products, arithmetic and copies ran while one was open for 3% of the time, Pallas kernels for 0%

commit v1 on v0

v1 whole, which is shorter than its diff:
```python
import functools

import jax
import jax.numpy as jnp
from jax import lax
from jax.experimental import pallas as pl
from jax.experimental.pallas import tpu as pltpu
from jax.sharding import Mesh
from jax.sharding import PartitionSpec as P


BANDS = 4
TILE = 512
STRIP = 16
WIDE = TILE * BANDS
CELLS = 16777216
BIG = 3e38
ALL = ("x", "zh", "z", "y", "c")
GROUP = ("z", "y", "c")
f32 = jnp.float32


Z, Y1, Y2, Y3, ZY1, ZY2, ZY3 = 8, 2, 4, 6, 10, 12, 14
PAIRS = [(ZY1, Y3), (Y1, ZY3), (ZY3, Y1), (Y3, ZY1), (Z, Y2), (Y2, Z), (ZY2, ZY2)]
SLOTS = []
for _a, _b in PAIRS:
    SLOTS += [(_a, _b), (_a | 1, _b | 1)]
SLOTS += [(1, 1), (0, 0)]
CHUNKS = [range(0, 4), range(4, 8), range(8, 12), range(12, 16)]


def position():
    z, y, c = (lax.axis_index(a) for a in GROUP)
    return z * 8 + y * 2 + c, c


def interleave(a, lane, pick):
    low = lane < 64
    even = (lane & 32) == 0
    u0 = jnp.where(low, a[0], pltpu.roll(a[2], 64, 1))
    u2 = jnp.where(low, pltpu.roll(a[0], 64, 1), a[2])
    u1 = jnp.where(low, a[1], pltpu.roll(a[3], 64, 1))
    u3 = jnp.where(low, pltpu.roll(a[1], 64, 1), a[3])
    v = [
        jnp.where(even, u0, pltpu.roll(u1, 32, 1)),
        jnp.where(even, pltpu.roll(u0, 96, 1), u1),
        jnp.where(even, u2, pltpu.roll(u3, 32, 1)),
        jnp.where(even, pltpu.roll(u2, 96, 1), u3),
    ]
    return [jnp.take_along_axis(t, pick, axis=1, mode="promise_in_bounds") for t in v]


def pieces_kernel(slots, first, last, *refs):
    refs = list(refs)
    px, fl = refs[:2]
    del refs[:2]
    acc_in = None if first else refs.pop(0)
    n = len(slots)
    outs = refs[:n]
    acc_out, pbuf, fbuf, sems = refs[n:]
    pos, core = position()
    copies = []
    for i, (k0, k1) in enumerate(slots):
        tile = pos ^ jnp.where(core == 0, k0, k1)
        cols = pl.ds(pl.multiple_of(tile * TILE, TILE), TILE)
        pair = (
            pltpu.make_async_copy(px.at[:, :, cols], pbuf.at[i], sems.at[0, i]),
            pltpu.make_async_copy(fl.at[:, :, cols], fbuf.at[i], sems.at[1, i]),
        )
        for copy in pair:
            copy.start()
        copies.append(pair)
    lane = lax.broadcasted_iota(jnp.int32, (8, 128), 1)
    pick = 32 * (lane & 3) + (lane >> 2)
    if first:
        acc = [jnp.full((8, 128), -BIG, f32)] * 8 + [jnp.zeros((8, 128), f32)] * 12
    else:
        acc = [acc_in[s] for s in range(20)]
    for i in range(n):
        for copy in copies[i]:
            copy.wait()
        for r in (0, 8):
            for s in range(TILE // 128):
                part = []
                for b in range(BANDS):
                    v = pbuf[i, b, r : r + 8, s * 128 : s * 128 + 128]
                    use = fbuf[i, b, r : r + 8, s * 128 : s * 128 + 128] == 1
                    m = jnp.where(use, v, 0.0)
                    acc[b] = jnp.maximum(acc[b], jnp.where(use, -v, -BIG))
                    acc[4 + b] = jnp.maximum(acc[4 + b], jnp.where(use, v, -BIG))
                    acc[8 + b] += jnp.where(use, 1.0, 0.0)
                    acc[12 + b] += m
                    acc[16 + b] += m * m
                    part.append(m)
                for j, o in enumerate(interleave(part, lane, pick)):
                    outs[i][r : r + 8, s * 512 + j * 128 : s * 512 + j * 128 + 128] = o
    if last:
        for s in range(20):
            reduce = jnp.max if s < 8 else jnp.sum
            acc_out[s : s + 1, :] = reduce(acc[s], axis=0, keepdims=True)
        acc_out[20:24, :] = jnp.zeros((4, 128), f32)
    else:
        for s in range(20):
            acc_out[s] = acc[s]


def pieces(slots, pixels, flags, acc, last):
    n = len(slots)
    first = acc is None
    any_ = pl.BlockSpec(memory_space=pltpu.HBM)
    vmem = pl.BlockSpec(memory_space=pltpu.VMEM)
    stat = jax.ShapeDtypeStruct((24, 128) if last else (20, 8, 128), f32)
    out = pl.pallas_call(
        functools.partial(pieces_kernel, slots, first, last),
        out_shape=[jax.ShapeDtypeStruct((STRIP, WIDE), f32)] * n + [stat],
        in_specs=[any_, any_] + ([] if first else [vmem]),
        out_specs=[vmem] * (n + 1),
        scratch_shapes=[
            pltpu.VMEM((n, BANDS, STRIP, TILE), f32),
            pltpu.VMEM((n, BANDS, STRIP, TILE), jnp.int32),
            pltpu.SemaphoreType.DMA((2, n)),
        ],
        compiler_params=pltpu.CompilerParams(vmem_limit_bytes=12 << 20),
        cost_estimate=pl.CostEstimate(flops=4_000_000, bytes_accessed=n * 393216, transcendentals=0),
    )(pixels, flags, *([] if first else [acc]))
    return out[:n], out[n]


def merged(a, b):
    row = lax.broadcasted_iota(jnp.int32, (24, 128), 0)
    return jnp.where(row < 8, jnp.maximum(a, b), a + b)


def assemble_kernel(slots, header, *refs):
    n = len(slots)
    refs = list(refs)
    if header:
        stats = refs[:8]
        del refs[:9]
    ins = refs[:n]
    out = refs[n]
    sems = refs[-1]
    pos, core = position()
    copies = []
    for i, (k0, k1) in enumerate(slots):
        key = jnp.where((core ^ (k0 & 1)) == 0, k0, k1)
        rows = pl.ds(pl.multiple_of((pos ^ key) * STRIP, STRIP), STRIP)
        copies.append(pltpu.make_async_copy(ins[i], out.at[0, rows, :], sems.at[i]))
        copies[-1].start()
    if header:
        head = refs[n + 1]
        top = stats[0][0:8, :]
        add = stats[0][8:24, :]
        for ref in stats[1:]:
            top = jnp.maximum(top, ref[0:8, :])
            add = add + ref[8:24, :]
        top = jnp.max(top, axis=1, keepdims=True)
        add = jnp.sum(add, axis=1, keepdims=True)
        count = add[0:4]
        divisor = jnp.maximum(count, 1.0)
        average = add[4:8] / divisor
        variance = add[8:12] / divisor - average * average
        columns = (-top[0:4], top[4:8], count / CELLS, average, jnp.sqrt(jnp.maximum(variance, 0.25)))
        for s, column in enumerate(columns):
            head[:, s : s + 1] = column
    for copy in copies:
        copy.wait()


def assemble(slots, ins, stats=None, half=None):
    header = stats is not None
    any_ = pl.BlockSpec(memory_space=pltpu.HBM)
    vmem = pl.BlockSpec(memory_space=pltpu.VMEM)
    n = len(slots)
    tile = jax.ShapeDtypeStruct((1, 256, WIDE), f32)
    return pl.pallas_call(
        functools.partial(assemble_kernel, slots, header),
        out_shape=[tile, jax.ShapeDtypeStruct((BANDS, 5), f32)] if header else tile,
        in_specs=([vmem] * 8 + [any_] if header else []) + [vmem] * n,
        out_specs=[any_, vmem] if header else any_,
        input_output_aliases={8: 0} if header else {},
        scratch_shapes=[pltpu.SemaphoreType.DMA((n,))],
        compiler_params=pltpu.CompilerParams(vmem_limit_bytes=12 << 20),
        cost_estimate=pl.CostEstimate(flops=1_000_000, bytes_accessed=n * 262144, transcendentals=0),
    )(*([*stats, half] if header else []), *ins)


def send(value, axes, size, keys):
    pairs = [(s, s ^ keys[s & 1]) for s in range(size)]
    return lax.ppermute(value, axes, pairs)


EARLY = 12


def on_device(pixels, flags):
    pixels = pltpu.with_memory_space_constraint(pixels, pltpu.HBM)
    flags = pltpu.with_memory_space_constraint(flags, pltpu.HBM)
    sent, acc = [], None
    for j, chunk in enumerate(CHUNKS):
        last = j == len(CHUNKS) - 1
        made, acc = pieces([SLOTS[i] for i in chunk], pixels, flags, acc, last)
        for i, piece in zip(chunk, made):
            sent.append(send(piece, GROUP, 16, SLOTS[i]) if SLOTS[i][0] else piece)
    s = acc
    s = merged(s, send(s, ("c",), 2, (1, 1)))
    s = merged(merged(s, send(s, ("x",), 4, (1, 1))), merged(send(s, ("x",), 4, (2, 2)), send(s, ("x",), 4, (3, 3))))
    s = merged(s, send(s, ("zh", "z"), 4, (3, 3)))
    stats = [s] + [send(s, ("z", "y"), 8, (k, k)) for k in range(1, 8)]
    order = list(range(15, 16)) + list(range(EARLY))
    half = assemble([SLOTS[i] for i in order], [sent[i] for i in order])
    order = list(range(EARLY, 15))
    tile, header = assemble([SLOTS[i] for i in order], [sent[i] for i in order], stats, half)
    return tile, header.T


def solution(mesh):
    split = Mesh(mesh.devices.reshape(4, 2, 2, 4, 2), ALL)
    placed = (P(None, ALL, None), P(None, ALL, None))
    return jax.shard_map(
        on_device, mesh=split, in_specs=placed, out_specs=(P(ALL, None, None), P()), check_vma=False
    )
```

time: 148 us -> 63.6 us (0.43)
  other arithmetic: 40.7 us -> 0.23 us
  blocking collectives: 35.4 us -> 0 us
  local copies, waits for them, and re-layouts: 32.7 us -> 0 us
  starting transfers between devices: 6.78 us -> 36.1 us
  waiting for transfers between devices: 31.5 us -> 15.4 us
  Pallas kernels: 0 us -> 11 us
    all_gather x4 -> x0, blocking collectives: 35.4 us -> none  [gathered_once(): both, at, found = (lax.all_gather(jnp.concatenate(lines), axis), 0, {})]
    ppermute x4 -> x27, starting transfers between devices: 6.78 us -> 36.1 us  [send(): return lax.ppermute(value, axes, pairs)]
    select_n x5 -> x3, other arithmetic: 27.3 us -> 0.22 us  [merged(): return jnp.where(row < 8, jnp.maximum(a, b), a + b)]
    ppermute x4 -> x27, waiting for transfers between devices: 31.5 us -> 15.4 us  [send(): return lax.ppermute(value, axes, pairs)]
    select_n x3 -> x0, local copies, waits for them, and re-layouts: 15.3 us -> none  [the longest x1 5.12 us: section_join(): new_upper = jnp.where(own_bit == 1, upper_half, incoming)]
    pallas_call x0 -> x6, Pallas kernels: none -> 11 us  [the longest x4 8.34 us: pieces(): pl.pallas_call(functools.partial(pieces_kernel, slots, first, last), out_...]
    reshape x1 -> x0, local copies, waits for them, and re-layouts: 10.7 us -> none  [on_device(): filled.reshape(band_total, strip_rows, members, TILE)]
    another operation x6 -> x0, other arithmetic: 6.38 us -> none  [section_join(): return jnp.stack([new_lower, new_upper], axis=1).reshape(result.shape)]
  transfers between devices with their start and end apart: 4 -> 27, of which waited for: 3 -> 11; matrix products, arithmetic and copies ran while one was open for 3% -> 0% of each run, Pallas kernels for 0% -> 2%
where the time goes in v1:
time: 63.6 us; the launch traced here: 63.4 us
  starting transfers between devices  36.1 us (57%)
  waiting for transfers between devices  15.4 us (24%)
  Pallas kernels  11 us (17%)
  between operations  0.72 us (1%)
    ppermute x27, starting transfers between devices, send(): return lax.ppermute(value, axes, pairs)  36.1 us
    ppermute x27, waiting for transfers between devices, send(): return lax.ppermute(value, axes, pairs)  15.4 us
    pallas_call x4, Pallas kernels, pieces(): pl.pallas_call(functools.partial(pieces_kernel, slots, first, last), out_...  8.34 us
    pallas_call x2, Pallas kernels, assemble(): pl.pallas_call(functools.partial(assemble_kernel, slots, header), out_sha...  2.65 us
  transfers between devices with their start and end apart: 27, of which 11 were waited for; matrix products, arithmetic and copies ran while one was open for 0% of the time, Pallas kernels for 2%

profile of v1, /device:TPU:0, one launch (start us, length us, event | category | flops | bytes accessed | tf_op | source)
XLA Modules:
  0.0 63.4 jit_solution(4047531621136504667)
XLA Ops:
  0.6 2.1 %shard_map.41 = (f32[16,2048]{1,0:T(8,128)S(1)}, f32[16,2048]{1,0:T(8,128)S(1)}, f32[16,2048]{1,0:T(8,128)S(1)}, f32[16,2048]{1,0:T(8,128)S(1)}, f32[20,8,128]{2,1,0:T(8,128)S(1)}) custom-call(f32[4,16,8192]{2,1,0:T(8,128)} %refs_0_.7, s32[4,16,8192]{2,1,0:T(8,128)} %refs_1_.7), custom_call_target="tpu_custom_call" | custom-call | flops 4000000 | bytes 1572864 | tf_op jit(solution)/shard_map/pallas_call | solution.py:113
  2.7 2.1 %shard_map.42 = (f32[16,2048]{1,0:T(8,128)S(1)}, f32[16,2048]{1,0:T(8,128)S(1)}, f32[16,2048]{1,0:T(8,128)S(1)}, f32[16,2048]{1,0:T(8,128)S(1)}, f32[20,8,128]{2,1,0:T(8,128)S(1)}) custom-call(f32[4,16,8192]{2,1,0:T(8,128)} %refs_0_.7, s32[4,16,8192]{2,1,0:T(8,128)} %refs_1_.7, f32[20,8,128]{2,1,0:T(8,128)S(1)} %get-tuple-element.24.refs_2_), custom_call_target="tpu_custom_call" | custom-call | flops 4000000 | bytes 1572864 | tf_op jit(solution)/shard_map/pallas_call | solution.py:113
  4.8 2.1 %shard_map.43 = (f32[16,2048]{1,0:T(8,128)S(1)}, f32[16,2048]{1,0:T(8,128)S(1)}, f32[16,2048]{1,0:T(8,128)S(1)}, f32[16,2048]{1,0:T(8,128)S(1)}, f32[20,8,128]{2,1,0:T(8,128)S(1)}) custom-call(f32[4,16,8192]{2,1,0:T(8,128)} %refs_0_.7, s32[4,16,8192]{2,1,0:T(8,128)} %refs_1_.7, f32[20,8,128]{2,1,0:T(8,128)S(1)} %get-tuple-element.25.refs_2_), custom_call_target="tpu_custom_call" | custom-call | flops 4000000 | bytes 1572864 | tf_op jit(solution)/shard_map/pallas_call | solution.py:113
  6.9 2.1 %shard_map.44 = (f32[16,2048]{1,0:T(8,128)S(1)}, f32[16,2048]{1,0:T(8,128)S(1)}, f32[16,2048]{1,0:T(8,128)S(1)}, f32[16,2048]{1,0:T(8,128)S(1)}, f32[24,128]{1,0:T(8,128)S(1)}) custom-call(f32[4,16,8192]{2,1,0:T(8,128)} %refs_0_.7, s32[4,16,8192]{2,1,0:T(8,128)} %refs_1_.7, f32[20,8,128]{2,1,0:T(8,128)S(1)} %get-tuple-element.26.refs_2_), custom_call_target="tpu_custom_call" | custom-call | flops 4000000 | bytes 1572864 | tf_op jit(solution)/shard_map/pallas_call | solution.py:113
  9.1 1.2 %collective-permute-done = f32[24,128]{1,0:T(8,128)S(1)} collective-permute-done((f32[24,128]{1,0:T(8,128)S(1)}, f32[24,128]{1,0:T(8,128)S(1)}, u32[]{:S(2)}, u32[]{:S(2)}) %collective-permute-start) | collective-permute-done | bytes 12320 | tf_op jit(solution)/shard_map/ppermute | solution.py:190
  10.3 3.2 %collective-permute-start.2 = (f32[24,128]{1,0:T(8,128)S(1)}, f32[24,128]{1,0:T(8,128)S(1)}, u32[]{:S(2)}, u32[]{:S(2)}) collective-permute-start(f32[24,128]{1,0:T(8,128)S(1)} %add_select_fusion.2), channel_id=1, source_target_pairs={{0,64},{32,96},{64,0},{96,32},{1,65},{33,97},{65,1},{97,33},{2,66}... | collective-permute-start | bytes 36872 | tf_op jit(solution)/shard_map/ppermute | solution.py:190
  15.5 2.8 %collective-permute-done.3 = f32[24,128]{1,0:T(8,128)S(1)} collective-permute-done((f32[24,128]{1,0:T(8,128)S(1)}, f32[24,128]{1,0:T(8,128)S(1)}, u32[]{:S(2)}, u32[]{:S(2)}) %collective-permute-start.3) | collective-permute-done | bytes 12320 | tf_op jit(solution)/shard_map/ppermute | solution.py:190
  18.5 4.1 %collective-permute-start.4 = (f32[24,128]{1,0:T(8,128)S(1)}, f32[24,128]{1,0:T(8,128)S(1)}, u32[]{:S(2)}, u32[]{:S(2)}) collective-permute-start(f32[24,128]{1,0:T(8,128)S(1)} %add_select_fusion.1), channel_id=1, source_target_pairs={{0,24},{8,16},{16,8},{24,0},{1,25},{9,17},{17,9},{25,1},{2,26},{10... | collective-permute-start | bytes 36872 | tf_op jit(solution)/shard_map/ppermute | solution.py:190
  22.5 1.7 %collective-permute-done.4 = f32[24,128]{1,0:T(8,128)S(1)} collective-permute-done((f32[24,128]{1,0:T(8,128)S(1)}, f32[24,128]{1,0:T(8,128)S(1)}, u32[]{:S(2)}, u32[]{:S(2)}) %collective-permute-start.4) | collective-permute-done | bytes 12320 | tf_op jit(solution)/shard_map/ppermute | solution.py:190
  24.3 2.4 %collective-permute-start.11 = (f32[24,128]{1,0:T(8,128)S(1)}, f32[24,128]{1,0:T(8,128)S(1)}, u32[]{:S(2)}, u32[]{:S(2)}) collective-permute-start(f32[24,128]{1,0:T(8,128)S(1)} %add_select_fusion.refs_0_), channel_id=1, source_target_pairs={{0,14},{2,12},{4,10},{6,8},{8,6},{10,4},{12,2},{14,0},{1,15},{3,13... | collective-permute-start | bytes 36872 | tf_op jit(solution)/shard_map/ppermute | solution.py:190
  26.6 2.2 %collective-permute-start.10 = (f32[24,128]{1,0:T(8,128)S(1)}, f32[24,128]{1,0:T(8,128)S(1)}, u32[]{:S(2)}, u32[]{:S(2)}) collective-permute-start(f32[24,128]{1,0:T(8,128)S(1)} %add_select_fusion.refs_0_), channel_id=1, source_target_pairs={{0,12},{2,14},{4,8},{6,10},{8,4},{10,6},{12,0},{14,2},{1,13},{3,15... | collective-permute-start | bytes 36872 | tf_op jit(solution)/shard_map/ppermute | solution.py:190
  29.2 2.6 %collective-permute-start.9 = (f32[24,128]{1,0:T(8,128)S(1)}, f32[24,128]{1,0:T(8,128)S(1)}, u32[]{:S(2)}, u32[]{:S(2)}) collective-permute-start(f32[24,128]{1,0:T(8,128)S(1)} %add_select_fusion.refs_0_), channel_id=1, source_target_pairs={{0,10},{2,8},{4,14},{6,12},{8,2},{10,0},{12,6},{14,4},{1,11},{3,9}... | collective-permute-start | bytes 36872 | tf_op jit(solution)/shard_map/ppermute | solution.py:190
  32.7 1.3 %collective-permute-start.7 = (f32[24,128]{1,0:T(8,128)S(1)}, f32[24,128]{1,0:T(8,128)S(1)}, u32[]{:S(2)}, u32[]{:S(2)}) collective-permute-start(f32[24,128]{1,0:T(8,128)S(1)} %add_select_fusion.refs_0_), channel_id=1, source_target_pairs={{0,6},{2,4},{4,2},{6,0},{8,14},{10,12},{12,10},{14,8},{1,7},{3,5},... | collective-permute-start | bytes 36872 | tf_op jit(solution)/shard_map/ppermute | solution.py:190
  35.3 1.5 %collective-permute-done.8.refs_4_ = f32[24,128]{1,0:T(8,128)S(1)} collective-permute-done((f32[24,128]{1,0:T(8,128)S(1)}, f32[24,128]{1,0:T(8,128)S(1)}, u32[]{:S(2)}, u32[]{:S(2)}) %collective-permute-start.8) | collective-permute-done | bytes 12320 | tf_op jit(solution)/shard_map/ppermute | solution.py:190
  37.7 2.8 %collective-permute-start.16 = (f32[16,2048]{1,0:T(8,128)S(1)}, f32[16,2048]{1,0:T(8,128)S(1)}, u32[]{:S(2)}, u32[]{:S(2)}) collective-permute-start(f32[16,2048]{1,0:T(8,128)S(1)} %get-tuple-element.33), channel_id=1, source_target_pairs={{0,14},{1,3},{2,12},{3,1},{4,10},{5,7},{6,8},{7,5},{8,6},{9,11},{1... | collective-permute-start | bytes 393224 | tf_op jit(solution)/shard_map/ppermute | solution.py:190
  40.9 1.8 %collective-permute-start.18 = (f32[16,2048]{1,0:T(8,128)S(1)}, f32[16,2048]{1,0:T(8,128)S(1)}, u32[]{:S(2)}, u32[]{:S(2)}) collective-permute-start(f32[16,2048]{1,0:T(8,128)S(1)} %get-tuple-element.35), channel_id=1, source_target_pairs={{0,6},{1,11},{2,4},{3,9},{4,2},{5,15},{6,0},{7,13},{8,14},{9,3},{1... | collective-permute-start | bytes 393224 | tf_op jit(solution)/shard_map/ppermute | solution.py:190
  43.3 2.2 %collective-permute-start.20 = (f32[16,2048]{1,0:T(8,128)S(1)}, f32[16,2048]{1,0:T(8,128)S(1)}, u32[]{:S(2)}, u32[]{:S(2)}) collective-permute-start(f32[16,2048]{1,0:T(8,128)S(1)} %get-tuple-element.37), channel_id=1, source_target_pairs={{0,8},{1,5},{2,10},{3,7},{4,12},{5,1},{6,14},{7,3},{8,0},{9,13},{1... | collective-permute-start | bytes 393224 | tf_op jit(solution)/shard_map/ppermute | solution.py:190
  48.3 1.7 %collective-permute-start.23 = (f32[16,2048]{1,0:T(8,128)S(1)}, f32[16,2048]{1,0:T(8,128)S(1)}, u32[]{:S(2)}, u32[]{:S(2)}) collective-permute-start(f32[16,2048]{1,0:T(8,128)S(1)} %get-tuple-element.40), channel_id=1, source_target_pairs={{0,5},{1,8},{2,7},{3,10},{4,1},{5,12},{6,3},{7,14},{8,13},{9,0},{1... | collective-permute-start | bytes 393224 | tf_op jit(solution)/shard_map/ppermute | solution.py:190
  50.0 2.2 %collective-permute-start.24 = (f32[16,2048]{1,0:T(8,128)S(1)}, f32[16,2048]{1,0:T(8,128)S(1)}, u32[]{:S(2)}, u32[]{:S(2)}) collective-permute-start(f32[16,2048]{1,0:T(8,128)S(1)} %get-tuple-element.41), channel_id=1, source_target_pairs={{0,12},{1,13},{2,14},{3,15},{4,8},{5,9},{6,10},{7,11},{8,4},{9,5},... | collective-permute-start | bytes 393224 | tf_op jit(solution)/shard_map/ppermute | solution.py:190
  53.3 1.5 %collective-permute-done.21.refs_10_ = f32[16,2048]{1,0:T(8,128)S(1)} collective-permute-done((f32[16,2048]{1,0:T(8,128)S(1)}, f32[16,2048]{1,0:T(8,128)S(1)}, u32[]{:S(2)}, u32[]{:S(2)}) %collective-permute-start.21) | collective-permute-done | bytes 131104 | tf_op jit(solution)/shard_map/ppermute | solution.py:190
  54.9 2.1 %collective-permute-start.6 = (f32[24,128]{1,0:T(8,128)S(1)}, f32[24,128]{1,0:T(8,128)S(1)}, u32[]{:S(2)}, u32[]{:S(2)}) collective-permute-start(f32[24,128]{1,0:T(8,128)S(1)} %add_select_fusion.refs_0_), channel_id=1, source_target_pairs={{0,4},{2,6},{4,0},{6,2},{8,12},{10,14},{12,8},{14,10},{1,5},{3,7},... | collective-permute-start | bytes 36872 | tf_op jit(solution)/shard_map/ppermute | solution.py:190
  58.0 1.3 %shard_map.45.refs_8_ = f32[1,256,2048]{2,1,0:T(8,128)} custom-call(f32[16,2048]{1,0:T(8,128)S(1)} %get-tuple-element.28.refs_0_, f32[16,2048]{1,0:T(8,128)S(1)} %collective-permute-done.12.refs_1_, f32[16,2048]{1,0:T(8,128)S(1)} %collective-permute-done.13.refs_2_, f32[16,2048]{1,0:T(8,128)S(1)} %collective-permute-done.14.refs_3_, ...), custom_call_target="tpu_custom_call" | custom-call | flops 1000000 | bytes 3407872 | tf_op jit(solution)/shard_map/pallas_call | solution.py:176
  59.3 2.7 %collective-permute-done.6.refs_2_ = f32[24,128]{1,0:T(8,128)S(1)} collective-permute-done((f32[24,128]{1,0:T(8,128)S(1)}, f32[24,128]{1,0:T(8,128)S(1)}, u32[]{:S(2)}, u32[]{:S(2)}) %collective-permute-start.6) | collective-permute-done | bytes 12320 | tf_op jit(solution)/shard_map/ppermute | solution.py:190
  62.1 1.4 %shard_map.46 = (f32[1,256,2048]{2,1,0:T(8,128)}, f32[4,5]{1,0:T(4,128)}) custom-call(f32[24,128]{1,0:T(8,128)S(1)} %add_select_fusion.refs_0_, f32[24,128]{1,0:T(8,128)S(1)} %collective-permute-done.5.refs_1_, f32[24,128]{1,0:T(8,128)S(1)} %collective-permute-done.6.refs_2_, ...), custom_call_target="tpu_custom_call", output_to_operand_aliasing={{0}: (8, {})} | custom-call | flops 1000000 | bytes 786432 | tf_op jit(solution)/shard_map/pallas_call | solution.py:176
  (40 shorter events, 11.8 us)
Async XLA Ops:
  10.3 5.2 %collective-permute-start.2 = (f32[24,128]{1,0:T(8,128)S(1)}, f32[24,128]{1,0:T(8,128)S(1)}, u32[]{:S(2)}, u32[]{:S(2)}) collective-permute-start(f32[24,128]{1,0:T(8,128)S(1)} %add_select_fusion.2), channel_id=1, source_target_pairs={{0,64},{32,96},{64,0},{96,32},{1,65},{33,97},{65,1},{97,33},{2,66}... | collective-permute-start | bytes 36872 | tf_op jit(solution)/shard_map/ppermute | solution.py:190
  18.5 5.7 %collective-permute-start.4 = (f32[24,128]{1,0:T(8,128)S(1)}, f32[24,128]{1,0:T(8,128)S(1)}, u32[]{:S(2)}, u32[]{:S(2)}) collective-permute-start(f32[24,128]{1,0:T(8,128)S(1)} %add_select_fusion.1), channel_id=1, source_target_pairs={{0,24},{8,16},{16,8},{24,0},{1,25},{9,17},{17,9},{25,1},{2,26},{10... | collective-permute-start | bytes 36872 | tf_op jit(solution)/shard_map/ppermute | solution.py:190
  24.3 7.7 %collective-permute-start.11 = (f32[24,128]{1,0:T(8,128)S(1)}, f32[24,128]{1,0:T(8,128)S(1)}, u32[]{:S(2)}, u32[]{:S(2)}) collective-permute-start(f32[24,128]{1,0:T(8,128)S(1)} %add_select_fusion.refs_0_), channel_id=1, source_target_pairs={{0,14},{2,12},{4,10},{6,8},{8,6},{10,4},{12,2},{14,0},{1,15},{3,13... | collective-permute-start | bytes 36872 | tf_op jit(solution)/shard_map/ppermute | solution.py:190
  26.6 6.1 %collective-permute-start.10 = (f32[24,128]{1,0:T(8,128)S(1)}, f32[24,128]{1,0:T(8,128)S(1)}, u32[]{:S(2)}, u32[]{:S(2)}) collective-permute-start(f32[24,128]{1,0:T(8,128)S(1)} %add_select_fusion.refs_0_), channel_id=1, source_target_pairs={{0,12},{2,14},{4,8},{6,10},{8,4},{10,6},{12,0},{14,2},{1,13},{3,15... | collective-permute-start | bytes 36872 | tf_op jit(solution)/shard_map/ppermute | solution.py:190
  28.8 11.7 %collective-permute-start.12 = (f32[16,2048]{1,0:T(8,128)S(1)}, f32[16,2048]{1,0:T(8,128)S(1)}, u32[]{:S(2)}, u32[]{:S(2)}) collective-permute-start(f32[16,2048]{1,0:T(8,128)S(1)} %get-tuple-element.29), channel_id=1, source_target_pairs={{0,10},{1,7},{2,8},{3,5},{4,14},{5,3},{6,12},{7,1},{8,2},{9,15},{1... | collective-permute-start | bytes 393224 | tf_op jit(solution)/shard_map/ppermute | solution.py:190
  29.2 5.7 %collective-permute-start.9 = (f32[24,128]{1,0:T(8,128)S(1)}, f32[24,128]{1,0:T(8,128)S(1)}, u32[]{:S(2)}, u32[]{:S(2)}) collective-permute-start(f32[24,128]{1,0:T(8,128)S(1)} %add_select_fusion.refs_0_), channel_id=1, source_target_pairs={{0,10},{2,8},{4,14},{6,12},{8,2},{10,0},{12,6},{14,4},{1,11},{3,9}... | collective-permute-start | bytes 36872 | tf_op jit(solution)/shard_map/ppermute | solution.py:190
  31.8 5.0 %collective-permute-start.8 = (f32[24,128]{1,0:T(8,128)S(1)}, f32[24,128]{1,0:T(8,128)S(1)}, u32[]{:S(2)}, u32[]{:S(2)}) collective-permute-start(f32[24,128]{1,0:T(8,128)S(1)} %add_select_fusion.refs_0_), channel_id=1, source_target_pairs={{0,8},{2,10},{4,12},{6,14},{8,0},{10,2},{12,4},{14,6},{1,9},{3,11}... | collective-permute-start | bytes 36872 | tf_op jit(solution)/shard_map/ppermute | solution.py:190
  32.0 8.9 %collective-permute-start.13 = (f32[16,2048]{1,0:T(8,128)S(1)}, f32[16,2048]{1,0:T(8,128)S(1)}, u32[]{:S(2)}, u32[]{:S(2)}) collective-permute-start(f32[16,2048]{1,0:T(8,128)S(1)} %get-tuple-element.30), channel_id=1, source_target_pairs={{0,11},{1,6},{2,9},{3,4},{4,15},{5,2},{6,13},{7,0},{8,3},{9,14},{1... | collective-permute-start | bytes 393224 | tf_op jit(solution)/shard_map/ppermute | solution.py:190
  32.7 5.0 %collective-permute-start.7 = (f32[24,128]{1,0:T(8,128)S(1)}, f32[24,128]{1,0:T(8,128)S(1)}, u32[]{:S(2)}, u32[]{:S(2)}) collective-permute-start(f32[24,128]{1,0:T(8,128)S(1)} %add_select_fusion.refs_0_), channel_id=1, source_target_pairs={{0,6},{2,4},{4,2},{6,0},{8,14},{10,12},{12,10},{14,8},{1,7},{3,5},... | collective-permute-start | bytes 36872 | tf_op jit(solution)/shard_map/ppermute | solution.py:190
  34.8 7.8 %collective-permute-start.14 = (f32[16,2048]{1,0:T(8,128)S(1)}, f32[16,2048]{1,0:T(8,128)S(1)}, u32[]{:S(2)}, u32[]{:S(2)}) collective-permute-start(f32[16,2048]{1,0:T(8,128)S(1)} %get-tuple-element.31), channel_id=1, source_target_pairs={{0,2},{1,15},{2,0},{3,13},{4,6},{5,11},{6,4},{7,9},{8,10},{9,7},{1... | collective-permute-start | bytes 393224 | tf_op jit(solution)/shard_map/ppermute | solution.py:190
  36.8 6.6 %collective-permute-start.15 = (f32[16,2048]{1,0:T(8,128)S(1)}, f32[16,2048]{1,0:T(8,128)S(1)}, u32[]{:S(2)}, u32[]{:S(2)}) collective-permute-start(f32[16,2048]{1,0:T(8,128)S(1)} %get-tuple-element.32), channel_id=1, source_target_pairs={{0,3},{1,14},{2,1},{3,12},{4,7},{5,10},{6,5},{7,8},{8,11},{9,6},{1... | collective-permute-start | bytes 393224 | tf_op jit(solution)/shard_map/ppermute | solution.py:190
  37.7 7.8 %collective-permute-start.16 = (f32[16,2048]{1,0:T(8,128)S(1)}, f32[16,2048]{1,0:T(8,128)S(1)}, u32[]{:S(2)}, u32[]{:S(2)}) collective-permute-start(f32[16,2048]{1,0:T(8,128)S(1)} %get-tuple-element.33), channel_id=1, source_target_pairs={{0,14},{1,3},{2,12},{3,1},{4,10},{5,7},{6,8},{7,5},{8,6},{9,11},{1... | collective-permute-start | bytes 393224 | tf_op jit(solution)/shard_map/ppermute | solution.py:190
  40.5 6.0 %collective-permute-start.17 = (f32[16,2048]{1,0:T(8,128)S(1)}, f32[16,2048]{1,0:T(8,128)S(1)}, u32[]{:S(2)}, u32[]{:S(2)}) collective-permute-start(f32[16,2048]{1,0:T(8,128)S(1)} %get-tuple-element.34), channel_id=1, source_target_pairs={{0,15},{1,2},{2,13},{3,0},{4,11},{5,6},{6,9},{7,4},{8,7},{9,10},{1... | collective-permute-start | bytes 393224 | tf_op jit(solution)/shard_map/ppermute | solution.py:190
  40.9 7.5 %collective-permute-start.18 = (f32[16,2048]{1,0:T(8,128)S(1)}, f32[16,2048]{1,0:T(8,128)S(1)}, u32[]{:S(2)}, u32[]{:S(2)}) collective-permute-start(f32[16,2048]{1,0:T(8,128)S(1)} %get-tuple-element.35), channel_id=1, source_target_pairs={{0,6},{1,11},{2,4},{3,9},{4,2},{5,15},{6,0},{7,13},{8,14},{9,3},{1... | collective-permute-start | bytes 393224 | tf_op jit(solution)/shard_map/ppermute | solution.py:190
  42.7 7.3 %collective-permute-start.19 = (f32[16,2048]{1,0:T(8,128)S(1)}, f32[16,2048]{1,0:T(8,128)S(1)}, u32[]{:S(2)}, u32[]{:S(2)}) collective-permute-start(f32[16,2048]{1,0:T(8,128)S(1)} %get-tuple-element.36), channel_id=1, source_target_pairs={{0,7},{1,10},{2,5},{3,8},{4,3},{5,14},{6,1},{7,12},{8,15},{9,2},{1... | collective-permute-start | bytes 393224 | tf_op jit(solution)/shard_map/ppermute | solution.py:190
  43.3 8.9 %collective-permute-start.20 = (f32[16,2048]{1,0:T(8,128)S(1)}, f32[16,2048]{1,0:T(8,128)S(1)}, u32[]{:S(2)}, u32[]{:S(2)}) collective-permute-start(f32[16,2048]{1,0:T(8,128)S(1)} %get-tuple-element.37), channel_id=1, source_target_pairs={{0,8},{1,5},{2,10},{3,7},{4,12},{5,1},{6,14},{7,3},{8,0},{9,13},{1... | collective-permute-start | bytes 393224 | tf_op jit(solution)/shard_map/ppermute | solution.py:190
  45.5 9.3 %collective-permute-start.21 = (f32[16,2048]{1,0:T(8,128)S(1)}, f32[16,2048]{1,0:T(8,128)S(1)}, u32[]{:S(2)}, u32[]{:S(2)}) collective-permute-start(f32[16,2048]{1,0:T(8,128)S(1)} %get-tuple-element.38), channel_id=1, source_target_pairs={{0,9},{1,4},{2,11},{3,6},{4,13},{5,0},{6,15},{7,2},{8,1},{9,12},{1... | collective-permute-start | bytes 393224 | tf_op jit(solution)/shard_map/ppermute | solution.py:190
  46.5 8.4 %collective-permute-start.22 = (f32[16,2048]{1,0:T(8,128)S(1)}, f32[16,2048]{1,0:T(8,128)S(1)}, u32[]{:S(2)}, u32[]{:S(2)}) collective-permute-start(f32[16,2048]{1,0:T(8,128)S(1)} %get-tuple-element.39), channel_id=1, source_target_pairs={{0,4},{1,9},{2,6},{3,11},{4,0},{5,13},{6,2},{7,15},{8,12},{9,1},{1... | collective-permute-start | bytes 393224 | tf_op jit(solution)/shard_map/ppermute | solution.py:190
  48.3 8.6 %collective-permute-start.23 = (f32[16,2048]{1,0:T(8,128)S(1)}, f32[16,2048]{1,0:T(8,128)S(1)}, u32[]{:S(2)}, u32[]{:S(2)}) collective-permute-start(f32[16,2048]{1,0:T(8,128)S(1)} %get-tuple-element.40), channel_id=1, source_target_pairs={{0,5},{1,8},{2,7},{3,10},{4,1},{5,12},{6,3},{7,14},{8,13},{9,0},{1... | collective-permute-start | bytes 393224 | tf_op jit(solution)/shard_map/ppermute | solution.py:190
  50.0 12.0 %collective-permute-start.24 = (f32[16,2048]{1,0:T(8,128)S(1)}, f32[16,2048]{1,0:T(8,128)S(1)}, u32[]{:S(2)}, u32[]{:S(2)}) collective-permute-start(f32[16,2048]{1,0:T(8,128)S(1)} %get-tuple-element.41), channel_id=1, source_target_pairs={{0,12},{1,13},{2,14},{3,15},{4,8},{5,9},{6,10},{7,11},{8,4},{9,5},... | collective-permute-start | bytes 393224 | tf_op jit(solution)/shard_map/ppermute | solution.py:190
  52.3 9.8 %collective-permute-start.25 = (f32[16,2048]{1,0:T(8,128)S(1)}, f32[16,2048]{1,0:T(8,128)S(1)}, u32[]{:S(2)}, u32[]{:S(2)}) collective-permute-start(f32[16,2048]{1,0:T(8,128)S(1)} %get-tuple-element.42), channel_id=1, source_target_pairs={{0,13},{1,12},{2,15},{3,14},{4,9},{5,8},{6,11},{7,10},{8,5},{9,4},... | collective-permute-start | bytes 393224 | tf_op jit(solution)/shard_map/ppermute | solution.py:190
  54.9 7.2 %collective-permute-start.26 = (f32[16,2048]{1,0:T(8,128)S(1)}, f32[16,2048]{1,0:T(8,128)S(1)}, u32[]{:S(2)}, u32[]{:S(2)}) collective-permute-start(f32[16,2048]{1,0:T(8,128)S(1)} %get-tuple-element.43), channel_id=1, source_target_pairs={{0,1},{1,0},{2,3},{3,2},{4,5},{5,4},{6,7},{7,6},{8,9},{9,8},{10,11... | collective-permute-start | bytes 393224 | tf_op jit(solution)/shard_map/ppermute | solution.py:190
  54.9 7.2 %collective-permute-start.6 = (f32[24,128]{1,0:T(8,128)S(1)}, f32[24,128]{1,0:T(8,128)S(1)}, u32[]{:S(2)}, u32[]{:S(2)}) collective-permute-start(f32[24,128]{1,0:T(8,128)S(1)} %add_select_fusion.refs_0_), channel_id=1, source_target_pairs={{0,4},{2,6},{4,0},{6,2},{8,12},{10,14},{12,8},{14,10},{1,5},{3,7},... | collective-permute-start | bytes 36872 | tf_op jit(solution)/shard_map/ppermute | solution.py:190
  56.9 5.1 %collective-permute-start.5 = (f32[24,128]{1,0:T(8,128)S(1)}, f32[24,128]{1,0:T(8,128)S(1)}, u32[]{:S(2)}, u32[]{:S(2)}) collective-permute-start(f32[24,128]{1,0:T(8,128)S(1)} %add_select_fusion.refs_0_), channel_id=1, source_target_pairs={{0,2},{2,0},{4,6},{6,4},{8,10},{10,8},{12,14},{14,12},{1,3},{3,1},... | collective-permute-start | bytes 36872 | tf_op jit(solution)/shard_map/ppermute | solution.py:190
  (3 other events, 9.9 us)

commit v2 on v1

v2 whole, which is shorter than its diff:
```python
import functools

import jax
import jax.numpy as jnp
from jax import lax
from jax.experimental import pallas as pl
from jax.experimental.pallas import tpu as pltpu
from jax.sharding import Mesh
from jax.sharding import PartitionSpec as P


BANDS = 4
TILE = 512
STRIP = 16
WIDE = TILE * BANDS
CELLS = 16777216
BIG = 3e38
ALL = ("x", "zh", "z", "y", "c")
GROUP = ("z", "y", "c")
f32 = jnp.float32


Z, Y1, Y2, Y3, ZY1, ZY2, ZY3 = 8, 2, 4, 6, 10, 12, 14
SLOTS = [(ZY1, Y3), (Y1, ZY3), (ZY3, Y1), (Y3, ZY1), (Z, Y2), (Y2, Z), (ZY2, ZY2)]
OWN = (0, 0)
BLOCK = STRIP * WIDE // 1024
STAT = 3


def other(keys):
    return (keys[0] ^ 1, keys[1] ^ 1)


def crossed(keys):
    return (keys[1] ^ 1, keys[0] ^ 1)


FIRST = [[k, other(k)] for k in SLOTS[:2]]
SECOND = [[k, other(k)] for k in SLOTS[2:6]] + [[SLOTS[6]], [other(SLOTS[6])], [other(OWN)], [OWN]]


def position():
    z, y, c = (lax.axis_index(a) for a in GROUP)
    return z * 8 + y * 2 + c, c


def interleave(a, lane, pick):
    low = lane < 64
    even = (lane & 32) == 0
    u0 = jnp.where(low, a[0], pltpu.roll(a[2], 64, 1))
    u2 = jnp.where(low, pltpu.roll(a[0], 64, 1), a[2])
    u1 = jnp.where(low, a[1], pltpu.roll(a[3], 64, 1))
    u3 = jnp.where(low, pltpu.roll(a[1], 64, 1), a[3])
    v = [
        jnp.where(even, u0, pltpu.roll(u1, 32, 1)),
        jnp.where(even, pltpu.roll(u0, 96, 1), u1),
        jnp.where(even, u2, pltpu.roll(u3, 32, 1)),
        jnp.where(even, pltpu.roll(u2, 96, 1), u3),
    ]
    return [jnp.take_along_axis(t, pick, axis=1, mode="promise_in_bounds") for t in v]


def pieces_kernel(plan, last, px, fl, *refs):
    refs = list(refs)
    before = refs.pop(0) if last else None
    outs = refs[: len(plan)]
    stat, pbuf, fbuf, sems = refs[len(plan) :]
    pos, core = position()
    order = [(out, h, keys) for out, pieces in zip(outs, plan) for h, keys in enumerate(pieces)]
    copies = []
    for i, (_, _, (k0, k1)) in enumerate(order):
        cols = pl.ds(pl.multiple_of((pos ^ jnp.where(core == 0, k0, k1)) * TILE, TILE), TILE)
        pair = (
            pltpu.make_async_copy(px.at[:, :, cols], pbuf.at[i], sems.at[0, i]),
            pltpu.make_async_copy(fl.at[:, :, cols], fbuf.at[i], sems.at[1, i]),
        )
        for copy in pair:
            copy.start()
        copies.append(pair)
    lane = lax.broadcasted_iota(jnp.int32, (8, 128), 1)
    pick = 32 * (lane & 3) + (lane >> 2)
    if last:
        acc = [before[s] for s in range(20)]
    else:
        acc = [jnp.full((8, 128), -BIG, f32)] * 8 + [jnp.zeros((8, 128), f32)] * 12
    for i, (out, h, _) in enumerate(order):
        for copy in copies[i]:
            copy.wait()
        for r in range(STRIP // 8):
            for s in range(TILE // 128):
                part = []
                for b in range(BANDS):
                    v = pbuf[i, b, r * 8 : r * 8 + 8, s * 128 : s * 128 + 128]
                    use = fbuf[i, b, r * 8 : r * 8 + 8, s * 128 : s * 128 + 128] == 1
                    m = jnp.where(use, v, 0.0)
                    acc[b] = jnp.maximum(acc[b], jnp.where(use, -v, -BIG))
                    acc[4 + b] = jnp.maximum(acc[4 + b], jnp.where(use, v, -BIG))
                    acc[8 + b] += jnp.where(use, 1.0, 0.0)
                    acc[12 + b] += m
                    acc[16 + b] += m * m
                    part.append(m)
                for j, o in enumerate(interleave(part, lane, pick)):
                    out[h * BLOCK + r * 16 + s * 4 + j] = o
    if not last:
        for s in range(20):
            stat[s] = acc[s]
        return
    zero = jnp.zeros((1, 128), f32)
    lines = [(jnp.max if s < 8 else jnp.sum)(a, axis=0, keepdims=True) for s, a in enumerate(acc)] + [zero] * 4
    for t in range(STAT):
        stat[t] = jnp.concatenate(lines[8 * t : 8 * t + 8], axis=0)


def pieces(plan, pixels, flags, before=None):
    hbm = pl.BlockSpec(memory_space=pltpu.HBM)
    vmem = pl.BlockSpec(memory_space=pltpu.VMEM)
    last = before is not None
    count = [len(keys) * BLOCK for keys in plan] + [STAT if last else 20]
    n = sum(len(keys) for keys in plan)
    return pl.pallas_call(
        functools.partial(pieces_kernel, plan, last),
        out_shape=[jax.ShapeDtypeStruct((c, 8, 128), f32) for c in count],
        in_specs=[hbm, hbm] + [vmem] * last,
        out_specs=[vmem] * len(count),
        scratch_shapes=[
            pltpu.VMEM((n, BANDS, STRIP, TILE), f32),
            pltpu.VMEM((n, BANDS, STRIP, TILE), jnp.int32),
            pltpu.SemaphoreType.DMA((2, n)),
        ],
        compiler_params=pltpu.CompilerParams(vmem_limit_bytes=12 << 20),
        cost_estimate=pl.CostEstimate(flops=n * 250_000, bytes_accessed=n * 393216, transcendentals=0),
    )(pixels, flags, *([before] if last else []))


def merged(a, b):
    tile = lax.broadcasted_iota(jnp.int32, (STAT, 8, 128), 0)
    return jnp.where(tile == 0, jnp.maximum(a, b), a + b)


def assemble_kernel(places, stats, half, *refs):
    refs = list(refs)
    stat = refs[:stats]
    ins = refs[stats + half : stats + half + len(places)]
    out, sems = refs[stats + half + len(places)], refs[-1]
    pos, core = position()
    copies = []
    for source, sources in zip(ins, places):
        for at, keys in enumerate(sources):
            if keys is None:
                continue
            rows = pl.ds(pl.multiple_of((pos ^ jnp.where(core == 0, *keys)) * BLOCK, BLOCK), BLOCK)
            part = source.at[at * BLOCK : (at + 1) * BLOCK]
            copies.append(pltpu.make_async_copy(part, out.at[rows], sems.at[len(copies)]))
            copies[-1].start()
    if stats:
        head = refs[-2]
        top = stat[0][0]
        add = [stat[0][1], stat[0][2]]
        for ref in stat[1:]:
            top = jnp.maximum(top, ref[0])
            add = [add[0] + ref[1], add[1] + ref[2]]
        top = jnp.max(top, axis=1, keepdims=True)
        add = [jnp.sum(a, axis=1, keepdims=True) for a in add]
        count = add[0][0:4]
        divisor = jnp.maximum(count, 1.0)
        average = add[0][4:8] / divisor
        variance = add[1][0:4] / divisor - average * average
        columns = (-top[0:4], top[4:8], count / CELLS, average, jnp.sqrt(jnp.maximum(variance, 0.25)))
        for s, column in enumerate(columns):
            head[:, s : s + 1] = column
    for copy in copies:
        copy.wait()


def assemble(pairs, half=None, stats=()):
    ins, places = [p[0] for p in pairs], [p[1] for p in pairs]
    hbm = pl.BlockSpec(memory_space=pltpu.HBM)
    vmem = pl.BlockSpec(memory_space=pltpu.VMEM)
    tile = jax.ShapeDtypeStruct((16 * BLOCK, 8, 128), f32)
    halves = [] if half is None else [half]
    return pl.pallas_call(
        functools.partial(assemble_kernel, places, len(stats), len(halves)),
        out_shape=[tile, jax.ShapeDtypeStruct((BANDS, 5), f32)] if stats else tile,
        in_specs=[vmem] * len(stats) + [hbm] * len(halves) + [vmem] * len(ins),
        out_specs=[hbm, vmem] if stats else hbm,
        input_output_aliases={len(stats): 0} if halves else {},
        scratch_shapes=[pltpu.SemaphoreType.DMA((16,))],
        compiler_params=pltpu.CompilerParams(vmem_limit_bytes=12 << 20),
        cost_estimate=pl.CostEstimate(flops=1_000_000, bytes_accessed=1 << 20, transcendentals=0),
    )(*stats, *halves, *ins)


def send(value, axes, size, keys):
    pairs = [(s, s ^ keys[s & 1]) for s in range(size)]
    return lax.ppermute(value, axes, pairs)


ROUNDS = [(("c",), 2, 1), (("x",), 4, 1), (("x",), 4, 3), (("zh", "z"), 4, 3)]
ASK = [(Z, Y1), (Y3, Y2), (ZY1, ZY3), (ZY2, ZY2)]


def on_device(pixels, flags):
    pixels = pltpu.with_memory_space_constraint(pixels, pltpu.HBM)
    flags = pltpu.with_memory_space_constraint(flags, pltpu.HBM)
    *made, stat = pieces(FIRST, pixels, flags)
    *more, theirs, mine, stat = pieces(SECOND, pixels, flags, stat)
    keys = SLOTS + [other(SLOTS[6])]
    got = [send(v, GROUP, 16, keys[i]) for i, v in enumerate(made + more)]
    swap = send(theirs, ("c",), 2, (1, 1))
    passed = []
    for j in (0, 3):
        halves = jnp.concatenate([got[i][BLOCK : 2 * BLOCK] for i in range(j, j + 3)], axis=0)
        passed.append(send(halves, ("c",), 2, (1, 1)))
    for axes, size, key in ROUNDS:
        stat = merged(stat, send(stat, axes, size, (key, key)))
    heard = [send(stat, GROUP, 16, k) for k in ASK]
    told = functools.reduce(merged, heard[:3])
    rest = send(told, ("c",), 2, (1, 1))
    landed = [(got[i], [SLOTS[i]]) for i in range(6)]
    relayed = [(v, [crossed(SLOTS[i]) for i in range(j, j + 3)]) for v, j in zip(passed, (0, 3))]
    ends = [(got[6], [keys[6]]), (got[7], [keys[7]])]
    half = assemble([(mine, [OWN]), (swap, [other(OWN)])] + landed[:3] + relayed[:1])
    tile, header = assemble(landed[3:] + relayed[1:] + ends, half, [stat, told, rest, heard[3]])
    tile = tile.reshape(1, 32, 16, 8, 128).transpose(0, 1, 3, 2, 4).reshape(1, 256, WIDE)
    return tile, header.T


def solution(mesh):
    split = Mesh(mesh.devices.reshape(4, 2, 2, 4, 2), ALL)
    placed = (P(None, ALL, None), P(None, ALL, None))
    return jax.shard_map(
        on_device, mesh=split, in_specs=placed, out_specs=(P(ALL, None, None), P()), check_vma=False
    )
```

time: 63.6 us -> 52.1 us (0.82)
  starting transfers between devices: 36.1 us -> 29.2 us
  waiting for transfers between devices: 15.4 us -> 11.6 us
  Pallas kernels: 11 us -> 9.24 us
    ppermute x27 -> x20, starting transfers between devices: 36.1 us -> 29.2 us  [send(): return lax.ppermute(value, axes, pairs)]
    ppermute x27 -> x20, waiting for transfers between devices: 15.4 us -> 11.6 us  [send(): return lax.ppermute(value, axes, pairs)]
    pallas_call x6 -> x4, Pallas kernels: 11 us -> 9.24 us  [the longest x2 6.38 us: pieces(): pl.pallas_call(functools.partial(pieces_kernel, plan, last), out_shape=[j...]
  transfers between devices with their start and end apart: 27 -> 20, of which waited for: 11 -> 6; matrix products, arithmetic and copies ran while one was open for 0% -> 1% of each run, Pallas kernels for 2% -> 2%
where the time goes in v2:
time: 52.1 us; the launch traced here: 51.4 us
  starting transfers between devices  29.2 us (56%)
  waiting for transfers between devices  11.6 us (22%)
  Pallas kernels  9.24 us (18%)
  between operations  0.79 us (2%)
    ppermute x20, starting transfers between devices, send(): return lax.ppermute(value, axes, pairs)  29.2 us
    ppermute x20, waiting for transfers between devices, send(): return lax.ppermute(value, axes, pairs)  11.6 us
    pallas_call x2, Pallas kernels, pieces(): pl.pallas_call(functools.partial(pieces_kernel, plan, last), out_shape=[j...  6.38 us
    pallas_call x2, Pallas kernels, assemble(): pl.pallas_call(functools.partial(assemble_kernel, places, len(stats), len...  2.86 us
  transfers between devices with their start and end apart: 20, of which 6 were waited for; matrix products, arithmetic and copies ran while one was open for 1% of the time, Pallas kernels for 2%

profile of v2, /device:TPU:0, one launch (start us, length us, event | category | flops | bytes accessed | tf_op | source)
XLA Modules:
  0.0 51.4 jit_solution(17265667562434732476)
XLA Ops:
  0.6 2.1 %shard_map.41 = (f32[64,8,128]{2,1,0:T(8,128)S(1)}, f32[64,8,128]{2,1,0:T(8,128)S(1)}, f32[20,8,128]{2,1,0:T(8,128)S(1)}) custom-call(f32[4,16,8192]{2,1,0:T(8,128)} %px.3, s32[4,16,8192]{2,1,0:T(8,128)} %fl.3), custom_call_target="tpu_custom_call" | custom-call | flops 1000000 | bytes 1572864 | tf_op jit(solution)/shard_map/pallas_call | solution.py:120
  2.7 4.3 %shard_map.42 = (f32[64,8,128]{2,1,0:T(8,128)S(1)}, f32[64,8,128]{2,1,0:T(8,128)S(1)}, f32[64,8,128]{2,1,0:T(8,128)S(1)}, f32[64,8,128]{2,1,0:T(8,128)S(1)}, f32...) custom-call(f32[4,16,8192]{2,1,0:T(8,128)} %px.3, ...), custom_call_target="tpu_custom_call" | custom-call | flops 3000000 | bytes 4718592 | tf_op jit(solution)/shard_map/pallas_call | solution.py:120
  7.1 3.2 %collective-permute-start.14 = (f32[64,8,128]{2,1,0:T(8,128)S(1)}, f32[64,8,128]{2,1,0:T(8,128)S(1)}, u32[]{:S(2)}, u32[]{:S(2)}) collective-permute-start(f32[64,8,128]{2,1,0:T(8,128)S(1)} %get-tuple-element.23), channel_id=1, source_target_pairs={{0,6},{1,11},{2,4},{3,9},{4,2},{5,15},{6,0},{7,13},{8,14},{9,3},{1... | collective-permute-start | bytes 786440 | tf_op jit(solution)/shard_map/ppermute | solution.py:195
  10.4 1.5 %collective-permute-start.1 = (f32[3,8,128]{2,1,0:T(8,128)S(1)}, f32[3,8,128]{2,1,0:T(8,128)S(1)}, u32[]{:S(2)}, u32[]{:S(2)}) collective-permute-start(f32[3,8,128]{2,1,0:T(8,128)S(1)} %add_select_fusion.4), channel_id=1, source_target_pairs={{0,32},{32,0},{64,96},{96,64},{1,33},{33,1},{65,97},{97,65},{2,34}... | collective-permute-start | bytes 36872 | tf_op jit(solution)/shard_map/ppermute | solution.py:195
  11.9 1.9 %collective-permute-start.15 = (f32[64,8,128]{2,1,0:T(8,128)S(1)}, f32[64,8,128]{2,1,0:T(8,128)S(1)}, u32[]{:S(2)}, u32[]{:S(2)}) collective-permute-start(f32[64,8,128]{2,1,0:T(8,128)S(1)} %get-tuple-element.24), channel_id=1, source_target_pairs={{0,8},{1,5},{2,10},{3,7},{4,12},{5,1},{6,14},{7,3},{8,0},{9,13},{1... | collective-permute-start | bytes 786440 | tf_op jit(solution)/shard_map/ppermute | solution.py:195
  13.8 1.3 %collective-permute-start.16 = (f32[64,8,128]{2,1,0:T(8,128)S(1)}, f32[64,8,128]{2,1,0:T(8,128)S(1)}, u32[]{:S(2)}, u32[]{:S(2)}) collective-permute-start(f32[64,8,128]{2,1,0:T(8,128)S(1)} %get-tuple-element.25), channel_id=1, source_target_pairs={{0,4},{1,9},{2,6},{3,11},{4,0},{5,13},{6,2},{7,15},{8,12},{9,1},{1... | collective-permute-start | bytes 786440 | tf_op jit(solution)/shard_map/ppermute | solution.py:195
  15.2 2.1 %collective-permute-start.2 = (f32[3,8,128]{2,1,0:T(8,128)S(1)}, f32[3,8,128]{2,1,0:T(8,128)S(1)}, u32[]{:S(2)}, u32[]{:S(2)}) collective-permute-start(f32[3,8,128]{2,1,0:T(8,128)S(1)} %add_select_fusion.3), channel_id=1, source_target_pairs={{0,96},{32,64},{64,32},{96,0},{1,97},{33,65},{65,33},{97,1},{2,98}... | collective-permute-start | bytes 36872 | tf_op jit(solution)/shard_map/ppermute | solution.py:195
  17.3 1.2 %collective-permute-start.10 = (f32[64,8,128]{2,1,0:T(8,128)S(1)}, f32[64,8,128]{2,1,0:T(8,128)S(1)}, u32[]{:S(2)}, u32[]{:S(2)}) collective-permute-start(f32[64,8,128]{2,1,0:T(8,128)S(1)} %get-tuple-element.20), channel_id=1, source_target_pairs={{0,10},{1,7},{2,8},{3,5},{4,14},{5,3},{6,12},{7,1},{8,2},{9,15},{1... | collective-permute-start | bytes 786440 | tf_op jit(solution)/shard_map/ppermute | solution.py:195
  18.5 1.6 %collective-permute-done.2 = f32[3,8,128]{2,1,0:T(8,128)S(1)} collective-permute-done((f32[3,8,128]{2,1,0:T(8,128)S(1)}, f32[3,8,128]{2,1,0:T(8,128)S(1)}, u32[]{:S(2)}, u32[]{:S(2)}) %collective-permute-start.2) | collective-permute-done | bytes 12320 | tf_op jit(solution)/shard_map/ppermute | solution.py:195
  20.1 0.7 %collective-permute-start.11 = (f32[64,8,128]{2,1,0:T(8,128)S(1)}, f32[64,8,128]{2,1,0:T(8,128)S(1)}, u32[]{:S(2)}, u32[]{:S(2)}) collective-permute-start(f32[64,8,128]{2,1,0:T(8,128)S(1)} %get-tuple-element.21), channel_id=1, source_target_pairs={{0,2},{1,15},{2,0},{3,13},{4,6},{5,11},{6,4},{7,9},{8,10},{9,7},{1... | collective-permute-start | bytes 786440 | tf_op jit(solution)/shard_map/ppermute | solution.py:195
  20.8 5.0 %collective-permute-start.12 = (f32[64,8,128]{2,1,0:T(8,128)S(1)}, f32[64,8,128]{2,1,0:T(8,128)S(1)}, u32[]{:S(2)}, u32[]{:S(2)}) collective-permute-start(f32[64,8,128]{2,1,0:T(8,128)S(1)} %get-tuple-element.22), channel_id=1, source_target_pairs={{0,14},{1,3},{2,12},{3,1},{4,10},{5,7},{6,8},{7,5},{8,6},{9,11},{1... | collective-permute-start | bytes 786440 | tf_op jit(solution)/shard_map/ppermute | solution.py:195
  25.8 1.9 %collective-permute-start.3 = (f32[3,8,128]{2,1,0:T(8,128)S(1)}, f32[3,8,128]{2,1,0:T(8,128)S(1)}, u32[]{:S(2)}, u32[]{:S(2)}) collective-permute-start(f32[3,8,128]{2,1,0:T(8,128)S(1)} %add_select_fusion.2), channel_id=1, source_target_pairs={{0,24},{8,16},{16,8},{24,0},{1,25},{9,17},{17,9},{25,1},{2,26},{10... | collective-permute-start | bytes 36872 | tf_op jit(solution)/shard_map/ppermute | solution.py:195
  27.9 2.4 %collective-permute-done.11.refs_3_ = f32[64,8,128]{2,1,0:T(8,128)S(1)} collective-permute-done((f32[64,8,128]{2,1,0:T(8,128)S(1)}, f32[64,8,128]{2,1,0:T(8,128)S(1)}, u32[]{:S(2)}, u32[]{:S(2)}) %collective-permute-start.11) | collective-permute-done | bytes 262176 | tf_op jit(solution)/shard_map/ppermute | solution.py:195
  30.3 1.0 %collective-permute-done.12.refs_4_ = f32[64,8,128]{2,1,0:T(8,128)S(1)} collective-permute-done((f32[64,8,128]{2,1,0:T(8,128)S(1)}, f32[64,8,128]{2,1,0:T(8,128)S(1)}, u32[]{:S(2)}, u32[]{:S(2)}) %collective-permute-start.12) | collective-permute-done | bytes 262176 | tf_op jit(solution)/shard_map/ppermute | solution.py:195
  31.6 2.1 %collective-permute-start.6 = (f32[3,8,128]{2,1,0:T(8,128)S(1)}, f32[3,8,128]{2,1,0:T(8,128)S(1)}, u32[]{:S(2)}, u32[]{:S(2)}) collective-permute-start(f32[3,8,128]{2,1,0:T(8,128)S(1)} %add_select_fusion.1.refs_0_), channel_id=1, source_target_pairs={{0,10},{1,15},{2,8},{3,13},{4,14},{5,11},{6,12},{7,9},{8,2},{9,7},... | collective-permute-start | bytes 36872 | tf_op jit(solution)/shard_map/ppermute | solution.py:195
  33.7 0.6 %collective-permute-start.5 = (f32[3,8,128]{2,1,0:T(8,128)S(1)}, f32[3,8,128]{2,1,0:T(8,128)S(1)}, u32[]{:S(2)}, u32[]{:S(2)}) collective-permute-start(f32[3,8,128]{2,1,0:T(8,128)S(1)} %add_select_fusion.1.refs_0_), channel_id=1, source_target_pairs={{0,6},{1,5},{2,4},{3,7},{4,2},{5,1},{6,0},{7,3},{8,14},{9,13},{10,... | collective-permute-start | bytes 36872 | tf_op jit(solution)/shard_map/ppermute | solution.py:195
  34.3 1.7 %collective-permute-start.4 = (f32[3,8,128]{2,1,0:T(8,128)S(1)}, f32[3,8,128]{2,1,0:T(8,128)S(1)}, u32[]{:S(2)}, u32[]{:S(2)}) collective-permute-start(f32[3,8,128]{2,1,0:T(8,128)S(1)} %add_select_fusion.1.refs_0_), channel_id=1, source_target_pairs={{0,8},{1,3},{2,10},{3,1},{4,12},{5,7},{6,14},{7,5},{8,0},{9,11},{1... | collective-permute-start | bytes 36872 | tf_op jit(solution)/shard_map/ppermute | solution.py:195
  36.7 1.9 %collective-permute-done.5 = f32[3,8,128]{2,1,0:T(8,128)S(1)} collective-permute-done((f32[3,8,128]{2,1,0:T(8,128)S(1)}, f32[3,8,128]{2,1,0:T(8,128)S(1)}, u32[]{:S(2)}, u32[]{:S(2)}) %collective-permute-start.5) | collective-permute-done | bytes 12320 | tf_op jit(solution)/shard_map/ppermute | solution.py:195
  38.6 1.0 %collective-permute-start.18 = (f32[32,8,128]{2,1,0:T(8,128)S(1)}, f32[32,8,128]{2,1,0:T(8,128)S(1)}, u32[]{:S(2)}, u32[]{:S(2)}) collective-permute-start(f32[32,8,128]{2,1,0:T(8,128)S(1)} %get-tuple-element.26), channel_id=1, source_target_pairs={{0,12},{1,13},{2,14},{3,15},{4,8},{5,9},{6,10},{7,11},{8,4},{9,5},... | collective-permute-start | bytes 393224 | tf_op jit(solution)/shard_map/ppermute | solution.py:195
  39.6 2.9 %collective-permute-start.19 = (f32[32,8,128]{2,1,0:T(8,128)S(1)}, f32[32,8,128]{2,1,0:T(8,128)S(1)}, u32[]{:S(2)}, u32[]{:S(2)}) collective-permute-start(f32[32,8,128]{2,1,0:T(8,128)S(1)} %get-tuple-element.27), channel_id=1, source_target_pairs={{0,13},{1,12},{2,15},{3,14},{4,9},{5,8},{6,11},{7,10},{8,5},{9,4},... | collective-permute-start | bytes 393224 | tf_op jit(solution)/shard_map/ppermute | solution.py:195
  42.5 0.9 %collective-permute-start.8 = (f32[3,8,128]{2,1,0:T(8,128)S(1)}, f32[3,8,128]{2,1,0:T(8,128)S(1)}, u32[]{:S(2)}, u32[]{:S(2)}) collective-permute-start(f32[3,8,128]{2,1,0:T(8,128)S(1)} %add_select_fusion.1.refs_0_), channel_id=1, source_target_pairs={{0,12},{1,13},{2,14},{3,15},{4,8},{5,9},{6,10},{7,11},{8,4},{9,5},... | collective-permute-start | bytes 36872 | tf_op jit(solution)/shard_map/ppermute | solution.py:195
  44.0 1.1 %shard_map.43.refs_4_ = f32[512,8,128]{2,1,0:T(8,128)} custom-call(f32[32,8,128]{2,1,0:T(8,128)S(1)} %get-tuple-element.18.refs_0_, f32[32,8,128]{2,1,0:T(8,128)S(1)} %collective-permute-done.9.refs_1_, f32[64,8,128]{2,1,0:T(8,128)S(1)} %collective-permute-done.10.refs_2_, f32[64,8,128]{2,1,0:T(8,128)S(1)} %collective-permute-done.11.refs_3_, ...), custom_call_target="tpu_custom_call" | custom-call | flops 1000000 | bytes 1048576 | tf_op jit(solution)/shard_map/pallas_call | solution.py:181
  45.1 4.5 %collective-permute-done.8.refs_3_ = f32[3,8,128]{2,1,0:T(8,128)S(1)} collective-permute-done((f32[3,8,128]{2,1,0:T(8,128)S(1)}, f32[3,8,128]{2,1,0:T(8,128)S(1)}, u32[]{:S(2)}, u32[]{:S(2)}) %collective-permute-start.8) | collective-permute-done | bytes 12320 | tf_op jit(solution)/shard_map/ppermute | solution.py:195
  49.6 1.8 %shard_map.44 = (f32[512,8,128]{2,1,0:T(8,128)}, f32[4,5]{1,0:T(4,128)}) custom-call(f32[3,8,128]{2,1,0:T(8,128)S(1)} %add_select_fusion.1.refs_0_, f32[3,8,128]{2,1,0:T(8,128)S(1)} %add_select_fusion.refs_1_, f32[3,8,128]{2,1,0:T(8,128)S(1)} %collective-permute-done.7.refs_2_, ...), custom_call_target="tpu_custom_call", output_to_operand_aliasing={{0}: (4, {})} | custom-call | flops 1000000 | bytes 1048576 | tf_op jit(solution)/shard_map/pallas_call | solution.py:181
  (34 shorter events, 2.1 us)
Async XLA Ops:
  7.0 3.3 %collective-permute-start = (f32[3,8,128]{2,1,0:T(8,128)S(1)}, f32[3,8,128]{2,1,0:T(8,128)S(1)}, u32[]{:S(2)}, u32[]{:S(2)}) collective-permute-start(f32[3,8,128]{2,1,0:T(8,128)S(1)} %get-tuple-element.17), channel_id=1, source_target_pairs={{0,1},{1,0},{2,3},{3,2},{4,5},{5,4},{6,7},{7,6},{8,9},{9,8},{10,11... | collective-permute-start | bytes 36872 | tf_op jit(solution)/shard_map/ppermute | solution.py:195
  7.1 13.7 %collective-permute-start.14 = (f32[64,8,128]{2,1,0:T(8,128)S(1)}, f32[64,8,128]{2,1,0:T(8,128)S(1)}, u32[]{:S(2)}, u32[]{:S(2)}) collective-permute-start(f32[64,8,128]{2,1,0:T(8,128)S(1)} %get-tuple-element.23), channel_id=1, source_target_pairs={{0,6},{1,11},{2,4},{3,9},{4,2},{5,15},{6,0},{7,13},{8,14},{9,3},{1... | collective-permute-start | bytes 786440 | tf_op jit(solution)/shard_map/ppermute | solution.py:195
  10.4 4.7 %collective-permute-start.1 = (f32[3,8,128]{2,1,0:T(8,128)S(1)}, f32[3,8,128]{2,1,0:T(8,128)S(1)}, u32[]{:S(2)}, u32[]{:S(2)}) collective-permute-start(f32[3,8,128]{2,1,0:T(8,128)S(1)} %add_select_fusion.4), channel_id=1, source_target_pairs={{0,32},{32,0},{64,96},{96,64},{1,33},{33,1},{65,97},{97,65},{2,34}... | collective-permute-start | bytes 36872 | tf_op jit(solution)/shard_map/ppermute | solution.py:195
  11.9 13.9 %collective-permute-start.15 = (f32[64,8,128]{2,1,0:T(8,128)S(1)}, f32[64,8,128]{2,1,0:T(8,128)S(1)}, u32[]{:S(2)}, u32[]{:S(2)}) collective-permute-start(f32[64,8,128]{2,1,0:T(8,128)S(1)} %get-tuple-element.24), channel_id=1, source_target_pairs={{0,8},{1,5},{2,10},{3,7},{4,12},{5,1},{6,14},{7,3},{8,0},{9,13},{1... | collective-permute-start | bytes 786440 | tf_op jit(solution)/shard_map/ppermute | solution.py:195
  13.8 13.9 %collective-permute-start.16 = (f32[64,8,128]{2,1,0:T(8,128)S(1)}, f32[64,8,128]{2,1,0:T(8,128)S(1)}, u32[]{:S(2)}, u32[]{:S(2)}) collective-permute-start(f32[64,8,128]{2,1,0:T(8,128)S(1)} %get-tuple-element.25), channel_id=1, source_target_pairs={{0,4},{1,9},{2,6},{3,11},{4,0},{5,13},{6,2},{7,15},{8,12},{9,1},{1... | collective-permute-start | bytes 786440 | tf_op jit(solution)/shard_map/ppermute | solution.py:195
  15.2 4.9 %collective-permute-start.2 = (f32[3,8,128]{2,1,0:T(8,128)S(1)}, f32[3,8,128]{2,1,0:T(8,128)S(1)}, u32[]{:S(2)}, u32[]{:S(2)}) collective-permute-start(f32[3,8,128]{2,1,0:T(8,128)S(1)} %add_select_fusion.3), channel_id=1, source_target_pairs={{0,96},{32,64},{64,32},{96,0},{1,97},{33,65},{65,33},{97,1},{2,98}... | collective-permute-start | bytes 36872 | tf_op jit(solution)/shard_map/ppermute | solution.py:195
  17.3 10.6 %collective-permute-start.10 = (f32[64,8,128]{2,1,0:T(8,128)S(1)}, f32[64,8,128]{2,1,0:T(8,128)S(1)}, u32[]{:S(2)}, u32[]{:S(2)}) collective-permute-start(f32[64,8,128]{2,1,0:T(8,128)S(1)} %get-tuple-element.20), channel_id=1, source_target_pairs={{0,10},{1,7},{2,8},{3,5},{4,14},{5,3},{6,12},{7,1},{8,2},{9,15},{1... | collective-permute-start | bytes 786440 | tf_op jit(solution)/shard_map/ppermute | solution.py:195
  20.1 10.2 %collective-permute-start.11 = (f32[64,8,128]{2,1,0:T(8,128)S(1)}, f32[64,8,128]{2,1,0:T(8,128)S(1)}, u32[]{:S(2)}, u32[]{:S(2)}) collective-permute-start(f32[64,8,128]{2,1,0:T(8,128)S(1)} %get-tuple-element.21), channel_id=1, source_target_pairs={{0,2},{1,15},{2,0},{3,13},{4,6},{5,11},{6,4},{7,9},{8,10},{9,7},{1... | collective-permute-start | bytes 786440 | tf_op jit(solution)/shard_map/ppermute | solution.py:195
  20.8 10.6 %collective-permute-start.12 = (f32[64,8,128]{2,1,0:T(8,128)S(1)}, f32[64,8,128]{2,1,0:T(8,128)S(1)}, u32[]{:S(2)}, u32[]{:S(2)}) collective-permute-start(f32[64,8,128]{2,1,0:T(8,128)S(1)} %get-tuple-element.22), channel_id=1, source_target_pairs={{0,14},{1,3},{2,12},{3,1},{4,10},{5,7},{6,8},{7,5},{8,6},{9,11},{1... | collective-permute-start | bytes 786440 | tf_op jit(solution)/shard_map/ppermute | solution.py:195
  25.8 5.7 %collective-permute-start.3 = (f32[3,8,128]{2,1,0:T(8,128)S(1)}, f32[3,8,128]{2,1,0:T(8,128)S(1)}, u32[]{:S(2)}, u32[]{:S(2)}) collective-permute-start(f32[3,8,128]{2,1,0:T(8,128)S(1)} %add_select_fusion.2), channel_id=1, source_target_pairs={{0,24},{8,16},{16,8},{24,0},{1,25},{9,17},{17,9},{25,1},{2,26},{10... | collective-permute-start | bytes 36872 | tf_op jit(solution)/shard_map/ppermute | solution.py:195
  27.8 21.8 %collective-permute-start.17 = (f32[96,8,128]{2,1,0:T(8,128)S(1)}, f32[96,8,128]{2,1,0:T(8,128)S(1)}, u32[]{:S(2)}, u32[]{:S(2)}) collective-permute-start(f32[96,8,128]{2,1,0:T(8,128)S(1)} %pad_maximum_fusion.1), channel_id=1, source_target_pairs={{0,1},{1,0},{2,3},{3,2},{4,5},{5,4},{6,7},{7,6},{8,9},{9,8},{10,11... | collective-permute-start | bytes 1179656 | tf_op jit(solution)/shard_map/ppermute | solution.py:195
  31.4 12.1 %collective-permute-start.13 = (f32[96,8,128]{2,1,0:T(8,128)S(1)}, f32[96,8,128]{2,1,0:T(8,128)S(1)}, u32[]{:S(2)}, u32[]{:S(2)}) collective-permute-start(f32[96,8,128]{2,1,0:T(8,128)S(1)} %pad_maximum_fusion), channel_id=1, source_target_pairs={{0,1},{1,0},{2,3},{3,2},{4,5},{5,4},{6,7},{7,6},{8,9},{9,8},{10,11... | collective-permute-start | bytes 1179656 | tf_op jit(solution)/shard_map/ppermute | solution.py:195
  31.6 4.6 %collective-permute-start.6 = (f32[3,8,128]{2,1,0:T(8,128)S(1)}, f32[3,8,128]{2,1,0:T(8,128)S(1)}, u32[]{:S(2)}, u32[]{:S(2)}) collective-permute-start(f32[3,8,128]{2,1,0:T(8,128)S(1)} %add_select_fusion.1.refs_0_), channel_id=1, source_target_pairs={{0,10},{1,15},{2,8},{3,13},{4,14},{5,11},{6,12},{7,9},{8,2},{9,7},... | collective-permute-start | bytes 36872 | tf_op jit(solution)/shard_map/ppermute | solution.py:195
  33.7 4.9 %collective-permute-start.5 = (f32[3,8,128]{2,1,0:T(8,128)S(1)}, f32[3,8,128]{2,1,0:T(8,128)S(1)}, u32[]{:S(2)}, u32[]{:S(2)}) collective-permute-start(f32[3,8,128]{2,1,0:T(8,128)S(1)} %add_select_fusion.1.refs_0_), channel_id=1, source_target_pairs={{0,6},{1,5},{2,4},{3,7},{4,2},{5,1},{6,0},{7,3},{8,14},{9,13},{10,... | collective-permute-start | bytes 36872 | tf_op jit(solution)/shard_map/ppermute | solution.py:195
  34.3 5.3 %collective-permute-start.4 = (f32[3,8,128]{2,1,0:T(8,128)S(1)}, f32[3,8,128]{2,1,0:T(8,128)S(1)}, u32[]{:S(2)}, u32[]{:S(2)}) collective-permute-start(f32[3,8,128]{2,1,0:T(8,128)S(1)} %add_select_fusion.1.refs_0_), channel_id=1, source_target_pairs={{0,8},{1,3},{2,10},{3,1},{4,12},{5,7},{6,14},{7,5},{8,0},{9,11},{1... | collective-permute-start | bytes 36872 | tf_op jit(solution)/shard_map/ppermute | solution.py:195
  36.2 6.4 %collective-permute-start.9 = (f32[32,8,128]{2,1,0:T(8,128)S(1)}, f32[32,8,128]{2,1,0:T(8,128)S(1)}, u32[]{:S(2)}, u32[]{:S(2)}) collective-permute-start(f32[32,8,128]{2,1,0:T(8,128)S(1)} %get-tuple-element.19), channel_id=1, source_target_pairs={{0,1},{1,0},{2,3},{3,2},{4,5},{5,4},{6,7},{7,6},{8,9},{9,8},{10,11... | collective-permute-start | bytes 393224 | tf_op jit(solution)/shard_map/ppermute | solution.py:195
  38.6 11.0 %collective-permute-start.18 = (f32[32,8,128]{2,1,0:T(8,128)S(1)}, f32[32,8,128]{2,1,0:T(8,128)S(1)}, u32[]{:S(2)}, u32[]{:S(2)}) collective-permute-start(f32[32,8,128]{2,1,0:T(8,128)S(1)} %get-tuple-element.26), channel_id=1, source_target_pairs={{0,12},{1,13},{2,14},{3,15},{4,8},{5,9},{6,10},{7,11},{8,4},{9,5},... | collective-permute-start | bytes 393224 | tf_op jit(solution)/shard_map/ppermute | solution.py:195
  39.6 10.0 %collective-permute-start.19 = (f32[32,8,128]{2,1,0:T(8,128)S(1)}, f32[32,8,128]{2,1,0:T(8,128)S(1)}, u32[]{:S(2)}, u32[]{:S(2)}) collective-permute-start(f32[32,8,128]{2,1,0:T(8,128)S(1)} %get-tuple-element.27), channel_id=1, source_target_pairs={{0,13},{1,12},{2,15},{3,14},{4,9},{5,8},{6,11},{7,10},{8,5},{9,4},... | collective-permute-start | bytes 393224 | tf_op jit(solution)/shard_map/ppermute | solution.py:195
  42.5 7.0 %collective-permute-start.8 = (f32[3,8,128]{2,1,0:T(8,128)S(1)}, f32[3,8,128]{2,1,0:T(8,128)S(1)}, u32[]{:S(2)}, u32[]{:S(2)}) collective-permute-start(f32[3,8,128]{2,1,0:T(8,128)S(1)} %add_select_fusion.1.refs_0_), channel_id=1, source_target_pairs={{0,12},{1,13},{2,14},{3,15},{4,8},{5,9},{6,10},{7,11},{8,4},{9,5},... | collective-permute-start | bytes 36872 | tf_op jit(solution)/shard_map/ppermute | solution.py:195
  43.5 6.1 %collective-permute-start.7 = (f32[3,8,128]{2,1,0:T(8,128)S(1)}, f32[3,8,128]{2,1,0:T(8,128)S(1)}, u32[]{:S(2)}, u32[]{:S(2)}) collective-permute-start(f32[3,8,128]{2,1,0:T(8,128)S(1)} %add_select_fusion.refs_1_), channel_id=1, source_target_pairs={{0,1},{1,0},{2,3},{3,2},{4,5},{5,4},{6,7},{7,6},{8,9},{9,8},{10,11... | collective-permute-start | bytes 36872 | tf_op jit(solution)/shard_map/ppermute | solution.py:195
